TPU v7x, 768 devices: a whole 4x8x12 slice. The times are simulated.
768 devices in a mesh: enc: 12 (over z), grp: 64 (over x, y, core).
Axes of the slice: x: 4, y: 8, z: 12, core: 2. Of those that a mesh axis runs over, the one named last changes fastest.
Arguments:
- patch_feats: bfloat16 [12, 4096, 8, 1152], P('enc', 'grp'), may hold values from -6 to 6
- windows: int32 [12, 4096, 3, 4], P('enc', 'grp'), may hold values from 0 to 7
- counts: int32 [12, 4096], P('enc', 'grp'), may hold values from 1 to 3
- owners: int32 [12, 4096], P('enc', 'grp'), may hold values from 0 to 63, as said below
- norm_gain: float32 [1152], replicated, may hold values from 0.1 to 1.9
- norm_bias: float32 [1152], replicated, may hold values from -1.8 to 1.8
- proj_weight: bfloat16 [1152, 4096], replicated, may hold values from -0.1875 to 0.1875
- proj_bias: float32 [4096], replicated, may hold values from -3 to 3
Outputs:
- projected: bfloat16 [12, 12288, 4096], P('enc', 'grp')
Inputs may be any that keep to these rules, and one draw needn't show every extreme that they name: `owners`: within each frame index, each aligned block of 64 clips (the clips of one device) names any section-0 rank at most 1 times, and some rank exactly 1 times.
All inputs are finite; a program needn't handle non-finite values.
Results may differ from a plain program's by a relative error of at most 0.0051.
Values may be sent and summed in bfloat16 or wider, within the bound.
A program may use at most 32 MiB of HBM per device.

v0:
```python
import jax
import jax.numpy as jnp
from jax import lax
from jax.sharding import PartitionSpec as P


def shifted(block, axis, distance):
    devices = range(lax.axis_size(axis))
    route = [(i - distance, i) for i in devices if i - distance in devices]
    return lax.ppermute(block, axis, route)


def pool_frame(frame_feats, frame_windows, norm_gain, norm_bias):
    values = frame_feats.astype(jnp.float32)
    average = jnp.mean(values, axis=-1, keepdims=True)
    spread = jnp.mean((values - average) ** 2, axis=-1, keepdims=True)
    normed = (values - average) * lax.rsqrt(spread + 1e-06) * norm_gain + norm_bias
    patch_ids = jnp.arange(frame_feats.shape[1], dtype=jnp.int32)
    selector = (
        jnp.sum((frame_windows[..., None] == patch_ids).astype(jnp.float32), axis=2)
        / frame_windows.shape[2]
    )
    pooled = jnp.einsum("cst,ctd->csd", selector, normed, precision=lax.Precision.HIGHEST)
    return pooled.astype(jnp.bfloat16)


def shards(patch_feats, windows, counts, owners, norm_gain, norm_bias, proj_weight, proj_bias):
    groups = lax.axis_size("grp")
    width = patch_feats.shape[3]
    pooled = pool_frame(patch_feats[0], windows[0], norm_gain, norm_bias)
    neighbour = shifted(pooled, "enc", -1)
    is_last = lax.axis_index("enc") == lax.axis_size("enc") - 1
    following = jnp.where(is_last, pooled, neighbour)
    merged = ((pooled.astype(jnp.float32) + following.astype(jnp.float32)) * 0.5).astype(
        jnp.bfloat16
    )
    samples = pooled.shape[0]
    per_sample = pooled.shape[1]
    most_per = -(-samples // groups)
    slot_rows = most_per * per_sample
    rows_out = groups * slot_rows
    count_row = counts[0]
    owner_row = owners[0]
    rank_ids = jnp.arange(groups, dtype=jnp.int32)
    matches = (owner_row[:, None] == rank_ids[None, :]).astype(jnp.int32)
    weighted = matches * count_row[:, None]
    earlier = jnp.cumsum(weighted, axis=0) - weighted
    within = jnp.sum(earlier * matches, axis=1)
    totals = jnp.sum(weighted, axis=0)
    step_index = jnp.arange(per_sample, dtype=jnp.int32)
    is_valid = step_index[None, :] < count_row[:, None]
    target = owner_row[:, None] * slot_rows + within[:, None] + step_index[None, :]
    target = jnp.where(is_valid, target, rows_out)
    token_ids = jnp.arange(samples * per_sample, dtype=jnp.int32)
    source = (
        jnp.full((rows_out + 1,), samples * per_sample, jnp.int32)
        .at[target.reshape(-1)]
        .set(token_ids)[:rows_out]
    )
    local_rows = merged.reshape(-1, width)
    row_width = local_rows.shape[1]
    flat_rows = jnp.concatenate([local_rows, jnp.zeros((1, row_width), jnp.bfloat16)], axis=0)
    outgoing = jnp.take(flat_rows, source, axis=0).reshape(groups, slot_rows, row_width)
    row_index = jnp.arange(rows_out, dtype=jnp.int32)
    received, arrived = (
        lax.all_to_all(outgoing, "grp", split_axis=0, concat_axis=0, tiled=True),
        lax.all_to_all(totals.reshape(groups, 1), "grp", split_axis=0, concat_axis=0, tiled=True),
    )
    arrived = arrived[:, 0]
    ending = jnp.cumsum(arrived)
    opening = ending - arrived
    sender = jnp.sum((ending[None, :] <= row_index[:, None]).astype(jnp.int32), axis=1)
    sender = jnp.minimum(sender, groups - 1)
    is_live = row_index < ending[-1]
    picked = sender * slot_rows + row_index - jnp.take(opening, sender)
    source_rows = jnp.where(is_live, picked, rows_out).astype(jnp.int32)
    gathered_rows = jnp.concatenate(
        [received.reshape(rows_out, row_width), jnp.zeros((1, row_width), jnp.bfloat16)], axis=0
    )
    packed = jnp.take(gathered_rows, source_rows, axis=0)
    product = jnp.dot(packed, proj_weight, preferred_element_type=jnp.float32)
    result = jnp.where(is_live[:, None], product + proj_bias, 0.0).astype(jnp.bfloat16)
    return result[None]


def solution(mesh):
    placed = (
        P("enc", "grp", None, None),
        P("enc", "grp", None, None),
        P("enc", "grp"),
        P("enc", "grp"),
        P(),
        P(),
        P(),
        P(),
    )
    return jax.shard_map(
        shards, mesh=mesh, in_specs=placed, out_specs=P("enc", "grp", None), check_vma=False
    )
```

profile of v0, /device:TPU:1, one launch (start us, length us, event | category | flops | bytes accessed | tf_op | source)
XLA Modules:
  0.0 77.6 jit_solution(5562090106585187935)
XLA Ops:
  0.0 0.8 %fusion.17 = s32[64,64]{1,0:T(8,128)S(1)} fusion(s32[64]{0:T(128)} %bitcast.32, s32[64]{0:T(128)} %bitcast.37), kind=kLoop, calls=%fused_computation.36 | loop fusion | flops 8192 | bytes 16896 | tf_op jit(solution)/shard_map/mul | solution.py:46
  1.0 0.9 %select_reduce_fusion = (s32[64]{0:T(128)S(1)}, s32[64]{0:T(128)S(1)}) fusion(s32[64,64]{1,0:T(8,128)S(1)} %reduce_window_sum.18, s32[64]{0:T(128)} %bitcast.33, s32[64]{0:T(128)} %bitcast.38), kind=kLoop, calls=%fused_computation.32 | loop fusion | flops 24448 | bytes 17408 | tf_op jit(solution)/shard_map/reduce_sum | solution.py:48
  1.8 0.7 copy.23
  2.5 14.5 %all-to-all-start = ((s32[64,1,1]{2,1,0:T(1,128)}), s32[64,1,1]{2,1,0:T(1,128)S(1)}, u32[]{:S(2)}, u32[]{:S(2)}) async-start(s32[64,1,1]{2,1,0:T(1,128)} %copy.23), calls=%async_computation | async-start | bytes 65536 | tf_op jit(solution)/shard_map/all_to_all | solution.py:67
  17.1 0.7 convert_reduce_fusion.2
  17.8 1.5 %convert_reduce_fusion = f32[64,8]{1,0:T(8,128)S(1)} fusion(bf16[1,64,8,1152]{3,2,1,0:T(8,128)(2,1)} %param.10), kind=kLoop, calls=%fused_computation.8 | loop fusion | flops 1179136 | bytes 1181696 | tf_op jit(solution)/shard_map/reduce_sum | solution.py:15
  19.3 0.4 fusion.6
  19.9 2.5 %convolution_convert_fusion = bf16[64,3,1152]{2,1,0:T(4,128)(2,1)S(1)} fusion(f32[64,3,8]{2,1,0:T(4,128)S(1)} %copy.25, bf16[1,64,8,1152]{3,2,1,0:T(8,128)(2,1)S(1)} %copy-done, f32[1152]{0:T(1024)S(1)} %copy-done.4, f32[1152]{0:T(1024)S(1)} %copy-done.5, f32[64,8]{1,0:T(8,128)S(1)} %add_rsqrt_fusion, f32[64,8]{1,0:T(8,128)S(1)} %broadcast_multiply_fusion), kind=kOutput, calls=%fused_computation.10 | convolution fusion | flops 24403968 | bytes 1641472 | tf_op jit(solution)/shard_map/cst,ctd->csd/dot_general | solution.py:23
  22.5 1.3 %collective-permute-start = (bf16[64,3,1152]{2,0,1:T(8,128)(2,1)S(1)}, bf16[64,3,1152]{2,0,1:T(8,128)(2,1)S(1)}, u32[]{:S(2)}, u32[]{:S(2)}) collective-permute-start(bf16[64,3,1152]{2,0,1:T(8,128)(2,1)S(1)} %copy.26), channel_id=1, source_target_pairs={{64,0},{128,64},{192,128},{256,192},{320,256},{384,320},{448,384},... | collective-permute-start | bytes 1327112 | tf_op jit(solution)/shard_map/ppermute | solution.py:10
  24.1 1.2 %scatter_custom_fusion = s32[193]{0:T(256)S(1)} fusion(s32[192]{0:T(256)S(1)} %bitcast.40, s32[192]{0:T(256)S(1)} %iota.27, s32[]{:T(128)} %constant.38.clone.1), kind=kCustom, calls=%fused_computation.56 | custom fusion | bytes 776 | tf_op jit(solution)/shard_map/scatter | solution.py:58
  25.3 1.1 %all-to-all-done = s32[64,1,1]{2,1,0:T(1,128)S(1)} async-done(((s32[64,1,1]{2,1,0:T(1,128)}), s32[64,1,1]{2,1,0:T(1,128)S(1)}, u32[]{:S(2)}, u32[]{:S(2)}) %all-to-all-start) | async-done | bytes 288 | tf_op jit(solution)/shard_map/all_to_all | solution.py:67
  26.5 0.6 slice.15
  27.2 1.2 %reduce.2 = s32[64]{0:T(128)S(1)} reduce(s32[64,1,1]{2,1,0:T(1,128)S(1)} %all-to-all-done, s32[]{:T(128)} %constant.24.clone.1), dimensions={1,2}, to_apply=%all_to_all.12.reduce_sub_computation | reduce | bytes 516 | tf_op jit(solution)/shard_map/all_to_all | solution.py:67
  28.5 7.0 %collective-permute-done = bf16[64,3,1152]{2,0,1:T(8,128)(2,1)S(1)} collective-permute-done((bf16[64,3,1152]{2,0,1:T(8,128)(2,1)S(1)}, bf16[64,3,1152]{2,0,1:T(8,128)(2,1)S(1)}, u32[]{:S(2)}, u32[]{:S(2)}) %collective-permute-start) | collective-permute-done | bytes 442400 | tf_op jit(solution)/shard_map/ppermute | solution.py:10
  35.5 0.5 multiply_convert_fusion
  36.1 0.4 reshape.138
  36.5 1.1 %gather_fusion.1 = bf16[192,1152]{1,0:T(8,128)(2,1)S(1)} fusion(bf16[193,1152]{1,0:T(8,128)(2,1)S(1)} %concatenate.6, s32[1024]{0:T(1024)S(1)} %pad_clamp_fusion.1), kind=kCustom, calls=%fused_computation.clone | custom fusion | bytes 885504 | tf_op jit(solution)/shard_map/jit(_take)/gather | solution.py:63
  37.7 1.0 %reshape.139 = bf16[64,3,1152]{2,1,0:T(4,128)(2,1)} reshape(bf16[192,1152]{1,0:T(8,128)(2,1)S(1)} %broadcast_select_fusion) | data formatting | bytes 884736 | tf_op jit(solution)/shard_map/reshape | solution.py:63
  38.7 11.5 %all-to-all-start.1 = ((bf16[64,3,1152]{2,1,0:T(4,128)(2,1)}), bf16[64,3,1152]{2,1,0:T(4,128)(2,1)S(1)}, u32[]{:S(2)}, u32[]{:S(2)}) async-start(bf16[64,3,1152]{2,1,0:T(4,128)(2,1)} %reshape.139), calls=%async_computation.1 | async-start | bytes 1179648 | tf_op jit(solution)/shard_map/all_to_all | solution.py:66
  50.3 1.6 %gather_fusion = s32[192]{0:T(256)S(1)} fusion(s32[64]{0:T(128)S(1)} %sub.24, s32[1024]{0:T(1024)S(1)} %pad_clamp_fusion.2), kind=kCustom, calls=%fused_computation.2 | custom fusion | bytes 2304 | tf_op jit(solution)/shard_map/jit(_take)/gather | solution.py:75
  51.8 0.7 compare_and_fusion
  52.5 16.4 %all-to-all-done.1 = bf16[64,3,1152]{2,1,0:T(4,128)(2,1)S(1)} async-done(((bf16[64,3,1152]{2,1,0:T(4,128)(2,1)}), bf16[64,3,1152]{2,1,0:T(4,128)(2,1)S(1)}, u32[]{:S(2)}, u32[]{:S(2)}) %all-to-all-start.1) | async-done | bytes 442400 | tf_op jit(solution)/shard_map/all_to_all | solution.py:66
  69.3 1.1 %gather_fusion.2 = bf16[192,1152]{1,0:T(8,128)(2,1)S(1)} fusion(bf16[193,1152]{1,0:T(8,128)(2,1)S(1)} %concatenate.7, s32[1024]{0:T(1024)S(1)} %pad_clamp_fusion), kind=kCustom, calls=%fused_computation.1.clone | custom fusion | bytes 885504 | tf_op jit(solution)/shard_map/jit(_take)/gather | solution.py:80
  70.4 7.1 %fusion.2 = bf16[1,192,4096]{2,1,0:T(8,128)(2,1)} fusion(bf16[1152,4096]{1,0:T(8,128)(2,1)} %param.16, f32[4096]{0:T(1024)S(1)} %copy-done.3, pred[192]{0:T(512)(128)(4,1)S(1)} %get-tuple-element.10, bf16[192,1152]{1,0:T(8,128)(2,1)S(1)} %gather_fusion.2, pred[192]{0:T(512)(128)(4,1)S(1)} %get-tuple-element.8), kind=kOutput, calls=%fused_computation.7 | convolution fusion | flops 1814519808 | bytes 11469184 | tf_op jit(solution)/shard_map/dot_general | solution.py:81
  (38 shorter events, 1.4 us)
Async XLA Ops:
  0.0 19.3 %copy-start = (bf16[1,64,8,1152]{3,2,1,0:T(8,128)(2,1)S(1)}, bf16[1,64,8,1152]{3,2,1,0:T(8,128)(2,1)}, u32[]{:S(2)}) copy-start(bf16[1,64,8,1152]{3,2,1,0:T(8,128)(2,1)} %param.10) | copy-start | bytes 3538948
  0.0 19.9 %copy-start.4 = (f32[1152]{0:T(1024)S(1)}, f32[1152]{0:T(1024)}, u32[]{:S(2)}) copy-start(f32[1152]{0:T(1024)} %param.15) | copy-start | bytes 13828
  0.0 19.9 %copy-start.5 = (f32[1152]{0:T(1024)S(1)}, f32[1152]{0:T(1024)}, u32[]{:S(2)}) copy-start(f32[1152]{0:T(1024)} %param.14) | copy-start | bytes 13828
  2.5 23.9 %all-to-all-start = ((s32[64,1,1]{2,1,0:T(1,128)}), s32[64,1,1]{2,1,0:T(1,128)S(1)}, u32[]{:S(2)}, u32[]{:S(2)}) async-start(s32[64,1,1]{2,1,0:T(1,128)} %copy.23), calls=%async_computation | async-start | bytes 65536 | tf_op jit(solution)/shard_map/all_to_all | solution.py:67
  19.7 4.1 %copy-start.2 = (s32[1,64]{1,0:T(1,128)S(1)}, s32[1,64]{1,0:T(1,128)}, u32[]{:S(2)}) copy-start(s32[1,64]{1,0:T(1,128)} %param.13) | copy-start | bytes 772
  19.7 4.1 %copy-start.1 = (s32[1,64]{1,0:T(1,128)S(1)}, s32[1,64]{1,0:T(1,128)}, u32[]{:S(2)}) copy-start(s32[1,64]{1,0:T(1,128)} %param.12) | copy-start | bytes 772
  22.5 13.1 %collective-permute-start = (bf16[64,3,1152]{2,0,1:T(8,128)(2,1)S(1)}, bf16[64,3,1152]{2,0,1:T(8,128)(2,1)S(1)}, u32[]{:S(2)}, u32[]{:S(2)}) collective-permute-start(bf16[64,3,1152]{2,0,1:T(8,128)(2,1)S(1)} %copy.26), channel_id=1, source_target_pairs={{64,0},{128,64},{192,128},{256,192},{320,256},{384,320},{448,384},... | collective-permute-start | bytes 1327112 | tf_op jit(solution)/shard_map/ppermute | solution.py:10
  38.7 30.2 %all-to-all-start.1 = ((bf16[64,3,1152]{2,1,0:T(4,128)(2,1)}), bf16[64,3,1152]{2,1,0:T(4,128)(2,1)S(1)}, u32[]{:S(2)}, u32[]{:S(2)}) async-start(bf16[64,3,1152]{2,1,0:T(4,128)(2,1)} %reshape.139), calls=%async_computation.1 | async-start | bytes 1179648 | tf_op jit(solution)/shard_map/all_to_all | solution.py:66
  69.3 1.2 %copy-start.3 = (f32[4096]{0:T(1024)S(1)}, f32[4096]{0:T(1024)}, u32[]{:S(2)}) copy-start(f32[4096]{0:T(1024)} %param.17) | copy-start | bytes 49156
where the time goes:
time: 78 us; the launch traced here: 77.6 us
  starting transfers between devices  27.3 us (35%)
  waiting for transfers between devices  24.4 us (31%)
  matrix products  9.64 us (12%)
  local copies, waits for them, and re-layouts  8.4 us (11%)
  other arithmetic  7.5 us (10%)
    all_to_all x1, waiting for transfers between devices, shards(): lax.all_to_all(outgoing, 'grp', split_axis=0, concat_axis=0, tiled=True)  16.4 us
    all_to_all x1, starting transfers between devices, shards(): lax.all_to_all(totals.reshape(groups, 1), 'grp', split_axis=0, concat_axi...  14.5 us
    all_to_all x1, starting transfers between devices, shards(): lax.all_to_all(outgoing, 'grp', split_axis=0, concat_axis=0, tiled=True)  11.5 us
    dot_general x1, matrix products, shards(): product = jnp.dot(packed, proj_weight, preferred_element_type=jnp.float32)  7.13 us
    ppermute x1, waiting for transfers between devices, shifted(): return lax.ppermute(block, axis, route)  6.99 us
    dot_general x1, matrix products, pool_frame(): jnp.einsum('cst,ctd->csd', selector, normed, precision=lax.Precision.HIGH...  2.52 us
  transfers between devices with their start and end apart: 3, of which 3 were waited for; matrix products, arithmetic and copies ran while one was open for 14% of the time, Pallas kernels for 0%

commit v1 on v0

v1 whole, which is shorter than its diff:
```python
import jax
import jax.numpy as jnp
from jax import lax
from jax.experimental import pallas as pl
from jax.experimental.pallas import tpu as pltpu
from jax.sharding import PartitionSpec as P

MESH = pl.DeviceIdType.MESH
F32 = jnp.float32
BF16 = jnp.bfloat16
LANES = 128
WIDTH = 1152
OUT_WIDTH = 4096
CLIPS = 64
PATCHES = 8
TOKENS = 3
RANKS = 64
ROWS = CLIPS * TOKENS
TILES = WIDTH // LANES
UNITS = ((0, 5), (1, 6), (2, 7), (3, 8), (4,))
PLACE = {tile: i for i, tile in enumerate(t for unit in UNITS for t in unit)}
ORDER = (4, 0, 1, 2, 3)
SLOT_TILES = 14


def iota(shape, dim):
    return lax.broadcasted_iota(jnp.int32, shape, dim)


def peer_of(step, me):
    x, y, core = me // 16, (me // 2) % 8, me % 2
    dx, dy, dcore = step // 16, (step // 2) % 8, step % 2
    return ((x + dx) % 4) * 16 + ((y + dy) % 8) * 2 + (core + dcore) % 2


def unit_tiles(unit):
    return 3 * unit, 3 if unit < 4 else 2


def exchange(
    feats_hbm, win_ref, counts_ref, owners_ref, gain_ref, bias_ref,
    packed_ref, live_ref,
    feats, stats, mine, theirs, outgoing, arrived,
    feat_sem, z_send, z_recv, x_send, x_recv, own_sem,
):
    me = lax.axis_index("grp")
    frame = lax.axis_index("enc")
    last = lax.axis_size("enc") - 1
    fetch = pltpu.make_async_copy(feats_hbm, feats, feat_sem)
    fetch.start()

    barrier = pltpu.get_barrier_semaphore()

    def greet(step, carry):
        pl.semaphore_signal(
            barrier, inc=1, device_id={"grp": peer_of(RANKS - step, me)}, device_id_type=MESH
        )
        return carry

    lax.fori_loop(1, RANKS, greet, 0)
    before = jnp.maximum(frame - 1, 0)
    after = jnp.minimum(frame + 1, last)

    @pl.when(frame > 0)
    def _():
        pl.semaphore_signal(barrier, inc=1, device_id={"enc": before}, device_id_type=MESH)

    @pl.when(frame < last)
    def _():
        pl.semaphore_signal(barrier, inc=1, device_id={"enc": after}, device_id_type=MESH)

    fetch.wait()
    group = 32

    def statistics(i, carry):
        at = pl.ds(pl.multiple_of(i * group, group), group)
        values = feats[at, :].astype(F32)
        mean = jnp.sum(values, axis=1, keepdims=True) * (1.0 / WIDTH)
        centred = values - mean
        var = jnp.sum(centred * centred, axis=1, keepdims=True) * (1.0 / WIDTH)
        stats[0, at, :] = jnp.broadcast_to(mean, (group, LANES))
        stats[1, at, :] = jnp.broadcast_to(lax.rsqrt(var + 1e-6), (group, LANES))
        return carry

    lax.fori_loop(0, CLIPS * PATCHES // group, statistics, 0)
    diagonal = iota((LANES, LANES), 0) == iota((LANES, LANES), 1)

    def as_row(which, start):
        column = stats[which, pl.ds(start, LANES), :]
        return jnp.sum(jnp.where(diagonal, column, 0.0), axis=0, keepdims=True)

    half = CLIPS // 2
    depth = half * PATCHES
    clip_diagonal = iota((CLIPS, CLIPS), 0) == iota((CLIPS, CLIPS), 1)

    def pick_column(token, w):
        row = win_ref[token, w : w + 1, :]
        return jnp.sum(jnp.where(clip_diagonal, row, 0), axis=1, keepdims=True)

    picked = [
        [pick_column(token, w) + PATCHES * (iota((CLIPS, 1), 0) % half) for w in range(4)]
        for token in range(TOKENS)
    ]
    for block in range(2):
        start = block * depth
        mean_row = jnp.concatenate([as_row(0, start), as_row(0, start + LANES)], axis=1)
        rstd_row = jnp.concatenate([as_row(1, start), as_row(1, start + LANES)], axis=1)
        parts = []
        for token in range(TOKENS):
            lanes = iota((half, depth), 1)
            weight = jnp.zeros((half, depth), F32)
            for w in range(4):
                picks = picked[token][w][block * half : (block + 1) * half]
                weight += jnp.where(picks == lanes, 0.25, 0.0)
            parts.append(weight)
        scaled = jnp.concatenate(parts, axis=0) * rstd_row
        shift = jnp.sum(scaled * mean_row, axis=1, keepdims=True)
        high = scaled.astype(BF16)
        rest = scaled - high.astype(F32)
        middle = rest.astype(BF16)
        low = (rest - middle.astype(F32)).astype(BF16)
        selector = jnp.concatenate([high, middle, low], axis=0)
        height = TOKENS * half
        for column in range(0, WIDTH, 2 * LANES):
            wide = min(2 * LANES, WIDTH - column)
            product = jnp.dot(
                selector, feats[pl.ds(start, depth), pl.ds(column, wide)],
                preferred_element_type=F32,
            )
            total = product[:height] + product[height : 2 * height] + product[2 * height :]
            pooled = (total - shift) * gain_ref[:, pl.ds(column, wide)]
            pooled = (pooled + bias_ref[:, pl.ds(column, wide)]).astype(BF16)
            for i in range(wide // LANES):
                place = PLACE[column // LANES + i]
                for token in range(TOKENS):
                    mine[place, pl.ds(token * CLIPS + block * half, half), :] = pooled[
                        token * half : (token + 1) * half, i * LANES : (i + 1) * LANES
                    ]

    @pl.when(frame == last)
    def _():
        theirs[...] = mine[...]

    owner_row = owners_ref[...]
    count_row = counts_ref[...].astype(F32)
    rank = iota((2 * RANKS, CLIPS), 0) // 2
    odd = iota((2 * RANKS, CLIPS), 0) % 2
    owned = jnp.where(owner_row == rank, 1.0, 0.0)
    even_rows = jnp.where(odd == 0, owned, 0.0)
    odd_rows = jnp.where(odd == 1, owned, 0.0)
    place_matrix = jnp.concatenate([even_rows, odd_rows], axis=1).astype(BF16)
    count_column = jnp.sum(odd_rows * count_row, axis=1, keepdims=True)

    neighbours = jnp.minimum(frame, 1) + jnp.minimum(last - frame, 1)
    pl.semaphore_wait(barrier, RANKS - 1 + neighbours)

    def shift_copy(unit):
        at = pl.ds(2 * unit, len(UNITS[unit]))
        return pltpu.make_async_remote_copy(
            mine.at[at], theirs.at[at], z_send.at[unit], z_recv.at[unit],
            device_id={"enc": before}, device_id_type=MESH,
        )

    @pl.when(frame > 0)
    def _():
        for unit in ORDER:
            shift_copy(unit).start()

    def own_copy(unit):
        at = pl.ds(*unit_tiles(unit))
        return pltpu.make_async_copy(
            outgoing.at[at, me], arrived.at[at, me], own_sem.at[unit]
        )

    for unit in ORDER:
        @pl.when(frame < last)
        def _():
            shift_copy(unit).wait_recv()

        merged = []
        for tile in UNITS[unit]:
            place = PLACE[tile]
            merged.append(
                ((mine[place].astype(F32) + theirs[place].astype(F32)) * 0.5).astype(BF16)
            )
        first, tiles = unit_tiles(unit)
        for i, block in enumerate(merged):
            spread = jnp.dot(place_matrix, block[: 2 * CLIPS], preferred_element_type=F32)
            outgoing[first + i] = spread.astype(BF16).reshape(RANKS, 2, LANES)
        if unit < 4:
            third = jnp.concatenate([block[2 * CLIPS :] for block in merged], axis=0)
            spread = jnp.dot(place_matrix, third, preferred_element_type=F32)
        else:
            spread = jnp.dot(
                even_rows.astype(BF16), merged[0][2 * CLIPS :], preferred_element_type=F32
            )
            spread = spread + count_column
        outgoing[first + tiles - 1] = spread.astype(BF16).reshape(RANKS, 2, LANES)
        own_copy(unit).start()

        def send(step, carry):
            peer = peer_of(RANKS - step, me)
            at = pl.ds(first, tiles)
            pltpu.make_async_remote_copy(
                outgoing.at[at, peer], arrived.at[at, me], x_send.at[unit], x_recv.at[unit],
                device_id={"grp": peer}, device_id_type=MESH,
            ).start()
            return carry

        lax.fori_loop(1, RANKS, send, 0)

    def arrival(unit, sem):
        at = pl.ds(*unit_tiles(unit))
        everyone = pl.ds(0, RANKS - 1)
        return pltpu.make_async_copy(
            outgoing.at[at, everyone], arrived.at[at, everyone], sem.at[unit]
        )

    for unit in ORDER:
        own_copy(unit).wait()
        arrival(unit, x_recv).wait()
        first, tiles = unit_tiles(unit)
        block = [arrived[first + i].reshape(2 * RANKS, LANES) for i in range(tiles)]
        if unit == 4:
            across = iota((2 * RANKS, 2 * RANKS), 1) // 2
            down = iota((2 * RANKS, 2 * RANKS), 0) // 2
            marked = iota((2 * RANKS, 2 * RANKS), 0) % 2 == 1
            earlier = jnp.where(marked & (down < across), 1.0, 0.0)
            same = jnp.where(marked & (down == across), 1.0, 0.0)
            table = jnp.concatenate([earlier, same], axis=1).astype(BF16)
            found = lax.dot_general(
                block[1], table, (((0,), (0,)), ((), ())), preferred_element_type=F32
            )
            opening = found[:1, : 2 * RANKS].astype(jnp.int32)
            count = found[:1, 2 * RANKS :].astype(jnp.int32)
            row = iota((ROWS, 2 * RANKS), 0)
            token = iota((ROWS, 2 * RANKS), 1) % 2
            pair = (row == opening + token) & (token < count)
            third = (row == opening + 2) & (count == 3)
            pair = jnp.where(pair, 1.0, 0.0)
            third_even = jnp.where(third & (token == 0), 1.0, 0.0)
            third_odd = jnp.where(third & (token == 1), 1.0, 0.0)
            live = jnp.sum(pair + third_even, axis=1, keepdims=True)
            live_ref[...] = jnp.broadcast_to(live, (ROWS, LANES))
            pack = (
                jnp.concatenate([pair, third_even], axis=1).astype(BF16),
                jnp.concatenate([pair, third_odd], axis=1).astype(BF16),
            )
        for i, tile in enumerate(UNITS[unit]):
            both = jnp.concatenate([block[i], block[tiles - 1]], axis=0)
            packed = jnp.dot(pack[i], both, preferred_element_type=F32).astype(BF16)
            packed_ref[:, tile * LANES : (tile + 1) * LANES] = packed

    for unit in ORDER:
        arrival(unit, x_send).wait()

    @pl.when(frame > 0)
    def _():
        for unit in ORDER:
            shift_copy(unit).wait_send()


def project(packed_ref, live_ref, weight_ref, bias_ref, result_ref, staged, sems):
    columns = staged.shape[2]
    shown = live_ref[:, :1] > 0.5

    def copy(n):
        at = pl.ds(n * columns, columns)
        return pltpu.make_async_copy(staged.at[n], result_ref.at[:, at], sems.at[n])

    for n in range(OUT_WIDTH // columns):
        at = pl.ds(n * columns, columns)
        product = jnp.dot(packed_ref[...], weight_ref[:, at], preferred_element_type=F32)
        staged[n] = jnp.where(shown, product + bias_ref[:, at], 0.0).astype(BF16)
        copy(n).start()
    for n in range(OUT_WIDTH // columns):
        copy(n).wait()


def shards(patch_feats, windows, counts, owners, norm_gain, norm_bias, proj_weight, proj_bias):
    vmem = pl.BlockSpec(memory_space=pltpu.VMEM)
    units = len(UNITS)
    packed, live = pl.pallas_call(
        exchange,
        name="exchange",
        out_shape=(
            jax.ShapeDtypeStruct((ROWS, WIDTH), BF16),
            jax.ShapeDtypeStruct((ROWS, LANES), F32),
        ),
        in_specs=[pl.BlockSpec(memory_space=pltpu.HBM)] + [vmem] * 5,
        out_specs=(vmem, vmem),
        scratch_shapes=[
            pltpu.VMEM((CLIPS * PATCHES, WIDTH), BF16),
            pltpu.VMEM((2, CLIPS * PATCHES, LANES), F32),
            pltpu.VMEM((TILES, ROWS, LANES), BF16),
            pltpu.VMEM((TILES, ROWS, LANES), BF16),
            pltpu.VMEM((SLOT_TILES, RANKS, 2, LANES), BF16),
            pltpu.VMEM((SLOT_TILES, RANKS, 2, LANES), BF16),
            pltpu.SemaphoreType.DMA,
        ] + [pltpu.SemaphoreType.DMA((units,))] * 5,
        compiler_params=pltpu.CompilerParams(
            collective_id=0, has_side_effects=True, vmem_limit_bytes=24 << 20
        ),
        cost_estimate=pl.CostEstimate(
            flops=60_000_000_000, bytes_accessed=4_000_000, transcendentals=0
        ),
    )(
        patch_feats.reshape(CLIPS * PATCHES, WIDTH), windows[0].transpose(1, 2, 0), counts, owners,
        norm_gain.reshape(1, WIDTH), norm_bias.reshape(1, WIDTH),
    )
    step = 512
    result = pl.pallas_call(
        project,
        name="project",
        out_shape=jax.ShapeDtypeStruct((ROWS, OUT_WIDTH), BF16),
        in_specs=[vmem] * 4,
        out_specs=pl.BlockSpec(memory_space=pltpu.HBM),
        scratch_shapes=[
            pltpu.VMEM((OUT_WIDTH // step, ROWS, step), BF16),
            pltpu.SemaphoreType.DMA((OUT_WIDTH // step,)),
        ],
        compiler_params=pltpu.CompilerParams(vmem_limit_bytes=24 << 20),
        cost_estimate=pl.CostEstimate(
            flops=2 * ROWS * WIDTH * OUT_WIDTH, bytes_accessed=12_000_000, transcendentals=0
        ),
    )(packed, live, proj_weight, proj_bias.reshape(1, OUT_WIDTH))
    return result[None]


def solution(mesh):
    placed = (
        P("enc", "grp", None, None),
        P("enc", "grp", None, None),
        P("enc", "grp"),
        P("enc", "grp"),
        P(),
        P(),
        P(),
        P(),
    )
    return jax.shard_map(
        shards, mesh=mesh, in_specs=placed, out_specs=P("enc", "grp", None), check_vma=False
    )
```

time: 78 us -> 42 us (0.54)
  the two profiles are of different devices: /device:TPU:1 before, /device:TPU:193 now
where the time goes in v1:
time: 42 us; the launch traced here: 41.8 us
  Pallas kernels  36.7 us (87%)
  local copies, waits for them, and re-layouts  5.02 us (12%)
    pallas_call x1, Pallas kernels, shards(): pl.pallas_call(exchange, name='exchange', out_shape=(jax.ShapeDtypeStruct...  33.7 us
    unnamed x16, local copies, waits for them, and re-layouts  3.47 us
    pallas_call x1, Pallas kernels, shards(): pl.pallas_call(project, name='project', out_shape=jax.ShapeDtypeStruct((R...  2.96 us
    reshape x1, local copies, waits for them, and re-layouts, shards(): norm_bias.reshape(1, WIDTH)  0.85 us

profile of v1, /device:TPU:193, one launch (start us, length us, event | category | flops | bytes accessed | tf_op | source)
XLA Modules:
  0.0 41.8 jit_solution(18057357663648446668)
XLA Ops:
  0.0 0.7 %reshape.13.gain_ref = f32[1,1152]{1,0:T(1,128)S(1)} reshape(f32[1152]{0:T(1024)} %param.12) | data formatting | bytes 9216 | tf_op jit(solution)/shard_map/reshape | solution.py:309
  0.7 0.0 slice-start
  0.7 0.8 %reshape.14.bias_ref = f32[1,1152]{1,0:T(1,128)S(1)} reshape(f32[1152]{0:T(1024)} %param.13) | data formatting | bytes 9216 | tf_op jit(solution)/shard_map/reshape | solution.py:309
  1.6 0.0 copy-start.1
  1.6 1.5 %copy-done.1 = bf16[1,64,8,1152]{3,2,1,0:T(8,128)(2,1)S(1)} copy-done((bf16[1,64,8,1152]{3,2,1,0:T(8,128)(2,1)S(1)}, bf16[1,64,8,1152]{3,2,1,0:T(8,128)(2,1)}, u32[]{:S(2)}) %copy-start.1) | copy-done | bytes 1179672
  3.0 0.0 copy-start.2
  3.0 0.7 %copy-done.2 = s32[1,64,3,4]{1,3,2,0:T(4,128)S(1)} copy-done((s32[1,64,3,4]{1,3,2,0:T(4,128)S(1)}, s32[1,64,3,4]{1,3,2,0:T(4,128)}, u32[]{:S(2)}) %copy-start.2) | copy-done | bytes 3096
  3.7 0.0 copy-start.3
  3.7 0.7 %copy-done.3 = s32[1,64]{1,0:T(1,128)S(1)} copy-done((s32[1,64]{1,0:T(1,128)S(1)}, s32[1,64]{1,0:T(1,128)}, u32[]{:S(2)}) %copy-start.3) | copy-done | bytes 280
  4.4 0.0 copy-start.4
  4.4 0.7 %copy-done.4 = s32[1,64]{1,0:T(1,128)S(1)} copy-done((s32[1,64]{1,0:T(1,128)S(1)}, s32[1,64]{1,0:T(1,128)}, u32[]{:S(2)}) %copy-start.4) | copy-done | bytes 280
  5.0 0.0 slice-start.1
  5.0 0.0 slice-start.2
  5.0 0.0 copy-start
  5.0 33.7 %exchange.1 = (bf16[192,1152]{1,0:T(8,128)(2,1)S(1)}, f32[192,128]{1,0:T(8,128)S(1)}) custom-call(bf16[512,1152]{1,0:T(8,128)(2,1)S(1)} %bitcast.9, s32[3,4,64]{2,1,0:T(4,128)S(1)} %bitcast.10, s32[1,64]{1,0:T(1,128)S(1)} %copy-done.3, s32[1,64]{1,0:T(1,128)S(1)} %copy-done.4, f32[1,1152]{1,0:T(1,128)S(1)} %reshape.13.gain_ref, f32[1,1152]{1,0:T(1,128)S(1)} %reshape.14.bias_ref), custom_call_target="tpu_custom_call" | custom-call | flops 60000002048 | bytes 4000000 | tf_op jit(solution)/shard_map/exchange/pallas_call | solution.py:283
  38.8 0.0 slice-done
  38.8 0.0 slice-done.1
  38.8 0.0 slice-done.2
  38.8 0.0 copy-done
  38.8 3.0 %project.1 = bf16[192,4096]{1,0:T(8,128)(2,1)} custom-call(bf16[192,1152]{1,0:T(8,128)(2,1)S(1)} %get-tuple-element.7.packed_ref, f32[192,128]{1,0:T(8,128)S(1)} %get-tuple-element.8.live_ref, bf16[1152,4096]{1,0:T(8,128)(2,1)S(1)} %bitcast.7, f32[1,4096]{1,0:T(1,128)S(1)} %bitcast.8), custom_call_target="tpu_custom_call" | custom-call | flops 1811939328 | bytes 12000000 | tf_op jit(solution)/shard_map/project/pallas_call | solution.py:312
  (1 shorter events, 0.0 us)
Async XLA Ops:
  0.7 38.1 %slice-start = ((s8[9437184]{0:T(1024)(128)(4,1)}), s8[4194304]{0:T(1024)(128)(4,1)S(1)}, s32[]{:S(2)}) async-start(s8[9437184]{0:T(1024)(128)(4,1)} %bitcast.6), calls=%async_computation | async-start | bytes 8388608
  1.6 1.5 %copy-start.1 = (bf16[1,64,8,1152]{3,2,1,0:T(8,128)(2,1)S(1)}, bf16[1,64,8,1152]{3,2,1,0:T(8,128)(2,1)}, u32[]{:S(2)}) copy-start(bf16[1,64,8,1152]{3,2,1,0:T(8,128)(2,1)} %param.8) | copy-start | bytes 3538948
  3.0 0.7 %copy-start.2 = (s32[1,64,3,4]{1,3,2,0:T(4,128)S(1)}, s32[1,64,3,4]{1,3,2,0:T(4,128)}, u32[]{:S(2)}) copy-start(s32[1,64,3,4]{1,3,2,0:T(4,128)} %param.9) | copy-start | bytes 9220
  3.7 0.7 %copy-start.3 = (s32[1,64]{1,0:T(1,128)S(1)}, s32[1,64]{1,0:T(1,128)}, u32[]{:S(2)}) copy-start(s32[1,64]{1,0:T(1,128)} %counts_ref.1) | copy-start | bytes 772
  4.4 0.7 %copy-start.4 = (s32[1,64]{1,0:T(1,128)S(1)}, s32[1,64]{1,0:T(1,128)}, u32[]{:S(2)}) copy-start(s32[1,64]{1,0:T(1,128)} %owners_ref.1) | copy-start | bytes 772
  5.0 33.8 %slice-start.1 = ((s8[9437184]{0:T(1024)(128)(4,1)}), s8[4194304]{0:T(1024)(128)(4,1)S(1)}, s32[]{:S(2)}) async-start(s8[9437184]{0:T(1024)(128)(4,1)} %bitcast.6), calls=%async_computation.1 | async-start | bytes 8388608
  5.0 33.8 %slice-start.2 = ((s8[9437184]{0:T(1024)(128)(4,1)}), s8[1048576]{0:T(1024)(128)(4,1)S(1)}, s32[]{:S(2)}) async-start(s8[9437184]{0:T(1024)(128)(4,1)} %bitcast.6), calls=%async_computation.2 | async-start | bytes 2097152
  5.0 33.8 %copy-start = (f32[4096]{0:T(1024)S(1)}, f32[4096]{0:T(1024)}, u32[]{:S(2)}) copy-start(f32[4096]{0:T(1024)} %param.15) | copy-start | bytes 49156

commit v2 on v1

--- a/solution.py
+++ b/solution.py
@@ -17,50 +17,75 @@
 RANKS = 64
 ROWS = CLIPS * TOKENS
 TILES = WIDTH // LANES
-UNITS = ((0, 5), (1, 6), (2, 7), (3, 8), (4,))
+UNITS = ((6,), (0, 3), (1, 4), (2, 5), (7,), (8,))
 PLACE = {tile: i for i, tile in enumerate(t for unit in UNITS for t in unit)}
-ORDER = (4, 0, 1, 2, 3)
-SLOT_TILES = 14
+FIRST = [sum(len(UNITS[v]) + 1 for v in range(u)) for u in range(len(UNITS))]
+SLOT_TILES = sum(len(unit) + 1 for unit in UNITS)
+LEADING = 7
+LEAD = LEADING * LANES
 
 
 def iota(shape, dim):
     return lax.broadcasted_iota(jnp.int32, shape, dim)
 
 
-def peer_of(step, me):
+def for_peers(me, act, loop):
     x, y, core = me // 16, (me // 2) % 8, me % 2
-    dx, dy, dcore = step // 16, (step // 2) % 8, step % 2
-    return ((x + dx) % 4) * 16 + ((y + dy) % 8) * 2 + (core + dcore) % 2
+    near = [
+        ((x + dx) % 4) * 16 + (core + dcore) % 2 for dx in (2, 1, 3, 0) for dcore in (0, 1)
+    ]
+
+    def row(i, carry):
+        dy = 4 + (1 - 2 * (i % 2)) * ((i + 1) // 2)
+        at = ((y + dy) % 8) * 2
+        for base in near:
+            act(base + at)
+        return carry
+
+    if loop:
+        lax.fori_loop(0, 7, row, 0)
+    else:
+        for i in range(7):
+            row(i, 0)
+    for i in (0, 1, 2, 3, 4, 5, 7):
+        act(near[i] + 2 * y)
 
 
 def unit_tiles(unit):
-    return 3 * unit, 3 if unit < 4 else 2
+    return FIRST[unit], len(UNITS[unit]) + 1
 
 
 def exchange(
-    feats_hbm, win_ref, counts_ref, owners_ref, gain_ref, bias_ref,
-    packed_ref, live_ref,
-    feats, stats, mine, theirs, outgoing, arrived,
-    feat_sem, z_send, z_recv, x_send, x_recv, own_sem,
+    feats_hbm, win_hbm, counts_hbm, owners_hbm, gain_hbm, bias_hbm, weight_hbm,
+    packed_ref, live_ref, total_ref, weight_ref,
+    feats, win_ref, counts_ref, owners_ref, gain_ref, bias_ref,
+    stats, mine, theirs, outgoing, arrived, leading,
+    fetch_sem, z_send, z_recv, x_send, x_recv, own_sem,
 ):
     me = lax.axis_index("grp")
     frame = lax.axis_index("enc")
     last = lax.axis_size("enc") - 1
-    fetch = pltpu.make_async_copy(feats_hbm, feats, feat_sem)
-    fetch.start()
+    pairs = (
+        (feats_hbm, feats), (win_hbm, win_ref), (counts_hbm, counts_ref),
+        (owners_hbm, owners_ref), (gain_hbm, gain_ref), (bias_hbm, bias_ref),
+        (weight_hbm, weight_ref),
+    )
+    fetches = [
+        pltpu.make_async_copy(source, target, fetch_sem.at[i])
+        for i, (source, target) in enumerate(pairs)
+    ]
+    for fetch in fetches[:-1]:
+        fetch.start()
 
     barrier = pltpu.get_barrier_semaphore()
-
-    def greet(step, carry):
-        pl.semaphore_signal(
-            barrier, inc=1, device_id={"grp": peer_of(RANKS - step, me)}, device_id_type=MESH
-        )
-        return carry
-
-    lax.fori_loop(1, RANKS, greet, 0)
     before = jnp.maximum(frame - 1, 0)
     after = jnp.minimum(frame + 1, last)
 
+    def greet(peer):
+        pl.semaphore_signal(barrier, inc=1, device_id={"grp": peer}, device_id_type=MESH)
+
+    for_peers(me, greet, False)
+
     @pl.when(frame > 0)
     def _():
         pl.semaphore_signal(barrier, inc=1, device_id={"enc": before}, device_id_type=MESH)
@@ -69,7 +94,9 @@
     def _():
         pl.semaphore_signal(barrier, inc=1, device_id={"enc": after}, device_id_type=MESH)
 
-    fetch.wait()
+    for fetch in fetches[:-1]:
+        fetch.wait()
+    fetches[-1].start()
     group = 32
 
     def statistics(i, carry):
@@ -128,14 +155,14 @@
                 preferred_element_type=F32,
             )
             total = product[:height] + product[height : 2 * height] + product[2 * height :]
-            pooled = (total - shift) * gain_ref[:, pl.ds(column, wide)]
-            pooled = (pooled + bias_ref[:, pl.ds(column, wide)]).astype(BF16)
+            total = total - shift
             for i in range(wide // LANES):
-                place = PLACE[column // LANES + i]
+                tile = column // LANES + i
+                pooled = total[:, i * LANES : (i + 1) * LANES] * gain_ref[tile : tile + 1, :]
+                pooled = (pooled + bias_ref[tile : tile + 1, :]).astype(BF16)
                 for token in range(TOKENS):
-                    mine[place, pl.ds(token * CLIPS + block * half, half), :] = pooled[
-                        token * half : (token + 1) * half, i * LANES : (i + 1) * LANES
-                    ]
+                    at = pl.ds(token * CLIPS + block * half, half)
+                    mine[PLACE[tile], at, :] = pooled[token * half : (token + 1) * half]
 
     @pl.when(frame == last)
     def _():
@@ -149,13 +176,14 @@
     even_rows = jnp.where(odd == 0, owned, 0.0)
     odd_rows = jnp.where(odd == 1, owned, 0.0)
     place_matrix = jnp.concatenate([even_rows, odd_rows], axis=1).astype(BF16)
+    third_matrix = even_rows.astype(BF16)
     count_column = jnp.sum(odd_rows * count_row, axis=1, keepdims=True)
 
     neighbours = jnp.minimum(frame, 1) + jnp.minimum(last - frame, 1)
     pl.semaphore_wait(barrier, RANKS - 1 + neighbours)
 
     def shift_copy(unit):
-        at = pl.ds(2 * unit, len(UNITS[unit]))
+        at = pl.ds(PLACE[UNITS[unit][0]], len(UNITS[unit]))
         return pltpu.make_async_remote_copy(
             mine.at[at], theirs.at[at], z_send.at[unit], z_recv.at[unit],
             device_id={"enc": before}, device_id_type=MESH,
@@ -163,7 +191,7 @@
 
     @pl.when(frame > 0)
     def _():
-        for unit in ORDER:
+        for unit in range(len(UNITS)):
             shift_copy(unit).start()
 
     def own_copy(unit):
@@ -172,7 +200,7 @@
             outgoing.at[at, me], arrived.at[at, me], own_sem.at[unit]
         )
 
-    for unit in ORDER:
+    for unit in range(len(UNITS)):
         @pl.when(frame < last)
         def _():
             shift_copy(unit).wait_recv()
@@ -187,27 +215,24 @@
         for i, block in enumerate(merged):
             spread = jnp.dot(place_matrix, block[: 2 * CLIPS], preferred_element_type=F32)
             outgoing[first + i] = spread.astype(BF16).reshape(RANKS, 2, LANES)
-        if unit < 4:
+        if tiles == 3:
             third = jnp.concatenate([block[2 * CLIPS :] for block in merged], axis=0)
             spread = jnp.dot(place_matrix, third, preferred_element_type=F32)
         else:
-            spread = jnp.dot(
-                even_rows.astype(BF16), merged[0][2 * CLIPS :], preferred_element_type=F32
-            )
-            spread = spread + count_column
+            spread = jnp.dot(third_matrix, merged[0][2 * CLIPS :], preferred_element_type=F32)
+            if unit == 0:
+                spread = spread + count_column
         outgoing[first + tiles - 1] = spread.astype(BF16).reshape(RANKS, 2, LANES)
         own_copy(unit).start()
 
-        def send(step, carry):
-            peer = peer_of(RANKS - step, me)
+        def send(peer):
             at = pl.ds(first, tiles)
             pltpu.make_async_remote_copy(
                 outgoing.at[at, peer], arrived.at[at, me], x_send.at[unit], x_recv.at[unit],
                 device_id={"grp": peer}, device_id_type=MESH,
             ).start()
-            return carry
-
-        lax.fori_loop(1, RANKS, send, 0)
+
+        for_peers(me, send, True)
 
     def arrival(unit, sem):
         at = pl.ds(*unit_tiles(unit))
@@ -216,12 +241,12 @@
             outgoing.at[at, everyone], arrived.at[at, everyone], sem.at[unit]
         )
 
-    for unit in ORDER:
+    for unit in range(len(UNITS)):
         own_copy(unit).wait()
         arrival(unit, x_recv).wait()
         first, tiles = unit_tiles(unit)
         block = [arrived[first + i].reshape(2 * RANKS, LANES) for i in range(tiles)]
-        if unit == 4:
+        if unit == 0:
             across = iota((2 * RANKS, 2 * RANKS), 1) // 2
             down = iota((2 * RANKS, 2 * RANKS), 0) // 2
             marked = iota((2 * RANKS, 2 * RANKS), 0) % 2 == 1
@@ -249,18 +274,30 @@
         for i, tile in enumerate(UNITS[unit]):
             both = jnp.concatenate([block[i], block[tiles - 1]], axis=0)
             packed = jnp.dot(pack[i], both, preferred_element_type=F32).astype(BF16)
-            packed_ref[:, tile * LANES : (tile + 1) * LANES] = packed
-
-    for unit in ORDER:
+            if tile < LEADING:
+                leading[:, tile * LANES : (tile + 1) * LANES] = packed
+            else:
+                at = (tile - LEADING) * LANES
+                packed_ref[:, at : at + LANES] = packed
+        if unit == 3:
+            fetches[-1].wait()
+            step = 512
+            for column in range(0, OUT_WIDTH, step):
+                at = pl.ds(column, step)
+                total_ref[:, at] = jnp.dot(
+                    leading[...], weight_ref[pl.ds(0, LEAD), at], preferred_element_type=F32
+                )
+
+    for unit in range(len(UNITS)):
         arrival(unit, x_send).wait()
 
     @pl.when(frame > 0)
     def _():
-        for unit in ORDER:
+        for unit in range(len(UNITS)):
             shift_copy(unit).wait_send()
 
 
-def project(packed_ref, live_ref, weight_ref, bias_ref, result_ref, staged, sems):
+def project(packed_ref, live_ref, total_ref, weight_ref, bias_ref, result_ref, staged, sems):
     columns = staged.shape[2]
     shown = live_ref[:, :1] > 0.5
 
@@ -270,7 +307,10 @@
 
     for n in range(OUT_WIDTH // columns):
         at = pl.ds(n * columns, columns)
-        product = jnp.dot(packed_ref[...], weight_ref[:, at], preferred_element_type=F32)
+        product = total_ref[:, at] + jnp.dot(
+            packed_ref[...], weight_ref[pl.ds(LEAD, WIDTH - LEAD), at],
+            preferred_element_type=F32,
+        )
         staged[n] = jnp.where(shown, product + bias_ref[:, at], 0.0).astype(BF16)
         copy(n).start()
     for n in range(OUT_WIDTH // columns):
@@ -279,24 +319,35 @@
 
 def shards(patch_feats, windows, counts, owners, norm_gain, norm_bias, proj_weight, proj_bias):
     vmem = pl.BlockSpec(memory_space=pltpu.VMEM)
+    hbm = pl.BlockSpec(memory_space=pltpu.HBM)
     units = len(UNITS)
-    packed, live = pl.pallas_call(
+    inputs = [
+        pltpu.with_memory_space_constraint(array, pltpu.HBM)
+        for array in (
+            patch_feats.reshape(CLIPS * PATCHES, WIDTH), windows[0].transpose(1, 2, 0),
+            counts, owners, norm_gain.reshape(TILES, LANES), norm_bias.reshape(TILES, LANES),
+            proj_weight,
+        )
+    ]
+    packed, live, total, weight = pl.pallas_call(
         exchange,
         name="exchange",
         out_shape=(
-            jax.ShapeDtypeStruct((ROWS, WIDTH), BF16),
+            jax.ShapeDtypeStruct((ROWS, WIDTH - LEAD), BF16),
             jax.ShapeDtypeStruct((ROWS, LANES), F32),
+            jax.ShapeDtypeStruct((ROWS, OUT_WIDTH), F32),
+            jax.ShapeDtypeStruct((WIDTH, OUT_WIDTH), BF16),
         ),
-        in_specs=[pl.BlockSpec(memory_space=pltpu.HBM)] + [vmem] * 5,
-        out_specs=(vmem, vmem),
-        scratch_shapes=[
-            pltpu.VMEM((CLIPS * PATCHES, WIDTH), BF16),
+        in_specs=[hbm] * len(inputs),
+        out_specs=(vmem,) * 4,
+        scratch_shapes=[pltpu.VMEM(array.shape, array.dtype) for array in inputs[:-1]] + [
             pltpu.VMEM((2, CLIPS * PATCHES, LANES), F32),
             pltpu.VMEM((TILES, ROWS, LANES), BF16),
             pltpu.VMEM((TILES, ROWS, LANES), BF16),
             pltpu.VMEM((SLOT_TILES, RANKS, 2, LANES), BF16),
             pltpu.VMEM((SLOT_TILES, RANKS, 2, LANES), BF16),
-            pltpu.SemaphoreType.DMA,
+            pltpu.VMEM((ROWS, LEAD), BF16),
+            pltpu.SemaphoreType.DMA((len(inputs),)),
         ] + [pltpu.SemaphoreType.DMA((units,))] * 5,
         compiler_params=pltpu.CompilerParams(
             collective_id=0, has_side_effects=True, vmem_limit_bytes=24 << 20
@@ -304,26 +355,23 @@
         cost_estimate=pl.CostEstimate(
             flops=60_000_000_000, bytes_accessed=4_000_000, transcendentals=0
         ),
-    )(
-        patch_feats.reshape(CLIPS * PATCHES, WIDTH), windows[0].transpose(1, 2, 0), counts, owners,
-        norm_gain.reshape(1, WIDTH), norm_bias.reshape(1, WIDTH),
-    )
+    )(*inputs)
     step = 512
     result = pl.pallas_call(
         project,
         name="project",
         out_shape=jax.ShapeDtypeStruct((ROWS, OUT_WIDTH), BF16),
-        in_specs=[vmem] * 4,
-        out_specs=pl.BlockSpec(memory_space=pltpu.HBM),
+        in_specs=[vmem] * 5,
+        out_specs=hbm,
         scratch_shapes=[
             pltpu.VMEM((OUT_WIDTH // step, ROWS, step), BF16),
             pltpu.SemaphoreType.DMA((OUT_WIDTH // step,)),
         ],
-        compiler_params=pltpu.CompilerParams(vmem_limit_bytes=24 << 20),
+        compiler_params=pltpu.CompilerParams(vmem_limit_bytes=16 << 20),
         cost_estimate=pl.CostEstimate(
             flops=2 * ROWS * WIDTH * OUT_WIDTH, bytes_accessed=12_000_000, transcendentals=0
         ),
-    )(packed, live, proj_weight, proj_bias.reshape(1, OUT_WIDTH))
+    )(packed, live, total, weight, proj_bias.reshape(1, OUT_WIDTH))
     return result[None]
 
 

time: 42 us -> 34.1 us (0.81)
  local copies, waits for them, and re-layouts: 5.02 us -> 0.01 us
  Pallas kernels: 36.7 us -> 33.9 us
    unnamed x16 -> x2, local copies, waits for them, and re-layouts: 3.47 us -> 0.01 us
    reshape x2 -> x0, local copies, waits for them, and re-layouts: 1.55 us -> none  [the longest x1 0.85 us: shards(): norm_bias.reshape(1, WIDTH)]
    pallas_call x1, Pallas kernels: 2.96 us -> 1.44 us  [shards(): pl.pallas_call(project, name='project', out_shape=jax.ShapeDtypeStruct((R...]
    pallas_call x1, Pallas kernels: 33.7 us -> 32.5 us  [shards(): pl.pallas_call(exchange, name='exchange', out_shape=(jax.ShapeDtypeStruct...]
where the time goes in v2:
time: 34.1 us; the launch traced here: 33.9 us
  Pallas kernels  33.9 us (99%)
    pallas_call x1, Pallas kernels, shards(): pl.pallas_call(exchange, name='exchange', out_shape=(jax.ShapeDtypeStruct...  32.5 us
    pallas_call x1, Pallas kernels, shards(): pl.pallas_call(project, name='project', out_shape=jax.ShapeDtypeStruct((R...  1.44 us

profile of v2, /device:TPU:193, one launch (start us, length us, event | category | flops | bytes accessed | tf_op | source)
XLA Modules:
  0.0 33.9 jit_solution(280488681288781502)
XLA Ops:
  0.0 0.0 copy-start
  0.0 32.5 %exchange.1 = (bf16[192,256]{1,0:T(8,128)(2,1)S(1)}, f32[192,128]{1,0:T(8,128)S(1)}, f32[192,4096]{1,0:T(8,128)S(1)}, bf16[1152,4096]{1,0:T(8,128)(2,1)S(1)}) custom-call(bf16[512,1152]{1,0:T(8,128)(2,1)} %bitcast.9, s32[3,4,64]{2,1,0:T(4,128)} %bitcast.12, s32[1,64]{1,0:T(1,128)} %counts_hbm.1, s32[1,64]{1,0:T(1,128)} %owners_hbm.1, f32[9,128]{1,0:T(8,128)} %bitcast.10, ...), custom_call_target="tpu_custom_call" | custom-call | flops 60000002048 | bytes 4000000 | tf_op jit(solution)/shard_map/exchange/pallas_call | solution.py:332
  32.5 0.0 copy-done
  32.5 1.4 %project.1 = bf16[192,4096]{1,0:T(8,128)(2,1)} custom-call(bf16[192,256]{1,0:T(8,128)(2,1)S(1)} %get-tuple-element.9.packed_ref, f32[192,128]{1,0:T(8,128)S(1)} %get-tuple-element.10.live_ref, f32[192,4096]{1,0:T(8,128)S(1)} %get-tuple-element.11.total_ref, bf16[1152,4096]{1,0:T(8,128)(2,1)S(1)} %get-tuple-element.12.weight_ref, f32[1,4096]{1,0:T(1,128)S(1)} %bitcast.8), custom_call_target="tpu_custom_call" | custom-call | flops 1811939328 | bytes 12000000 | tf_op jit(solution)/shard_map/project/pallas_call | solution.py:360
Async XLA Ops:
  0.0 32.5 %copy-start = (f32[4096]{0:T(1024)S(1)}, f32[4096]{0:T(1024)}, u32[]{:S(2)}) copy-start(f32[4096]{0:T(1024)} %param.15) | copy-start | bytes 49156

commit v3 on v2

--- a/solution.py
+++ b/solution.py
@@ -17,10 +17,18 @@
 RANKS = 64
 ROWS = CLIPS * TOKENS
 TILES = WIDTH // LANES
-UNITS = ((6,), (0, 3), (1, 4), (2, 5), (7,), (8,))
-PLACE = {tile: i for i, tile in enumerate(t for unit in UNITS for t in unit)}
-FIRST = [sum(len(UNITS[v]) + 1 for v in range(u)) for u in range(len(UNITS))]
-SLOT_TILES = sum(len(unit) + 1 for unit in UNITS)
+GROUPS = (
+    ((6,), (6,), 0, 2),
+    ((0, 3), (0, 3), 2, 3),
+    ((1, 4), (1, 4), 5, 3),
+    ((2, 5), (2, 5), 8, 3),
+    ((7,), (), 11, 1),
+    ((8,), (7, 8), 12, 2),
+)
+PLACE = {tile: i for i, tile in enumerate(t for group in GROUPS for t in group[0])}
+PAIR_AT = {tile: g[2] + i for g in GROUPS for i, tile in enumerate(g[0])}
+SLOT_TILES = 14
+PIECE = 32
 LEADING = 7
 LEAD = LEADING * LANES
 
@@ -49,10 +57,6 @@
             row(i, 0)
     for i in (0, 1, 2, 3, 4, 5, 7):
         act(near[i] + 2 * y)
-
-
-def unit_tiles(unit):
-    return FIRST[unit], len(UNITS[unit]) + 1
 
 
 def exchange(
@@ -182,71 +186,75 @@
     neighbours = jnp.minimum(frame, 1) + jnp.minimum(last - frame, 1)
     pl.semaphore_wait(barrier, RANKS - 1 + neighbours)
 
-    def shift_copy(unit):
-        at = pl.ds(PLACE[UNITS[unit][0]], len(UNITS[unit]))
-        return pltpu.make_async_remote_copy(
-            mine.at[at], theirs.at[at], z_send.at[unit], z_recv.at[unit],
-            device_id={"enc": before}, device_id_type=MESH,
-        )
+    pieces = ROWS // PIECE
 
     @pl.when(frame > 0)
     def _():
-        for unit in range(len(UNITS)):
-            shift_copy(unit).start()
-
-    def own_copy(unit):
-        at = pl.ds(*unit_tiles(unit))
-        return pltpu.make_async_copy(
-            outgoing.at[at, me], arrived.at[at, me], own_sem.at[unit]
-        )
-
-    for unit in range(len(UNITS)):
-        @pl.when(frame < last)
-        def _():
-            shift_copy(unit).wait_recv()
-
-        merged = []
-        for tile in UNITS[unit]:
+        def shift(i, carry):
+            place = i // pieces
+            at = pl.ds(pl.multiple_of((i % pieces) * PIECE, PIECE), PIECE)
+            pltpu.make_async_remote_copy(
+                mine.at[place, at], theirs.at[place, at], z_send.at[place], z_recv.at[place],
+                device_id={"enc": before}, device_id_type=MESH,
+            ).start()
+            return carry
+
+        lax.fori_loop(0, TILES * pieces, shift, 0)
+
+    def own_copy(i):
+        at = pl.ds(*GROUPS[i][2:])
+        return pltpu.make_async_copy(outgoing.at[at, me], arrived.at[at, me], own_sem.at[i])
+
+    merged = {}
+    for i, (tiles, thirds, first, depth) in enumerate(GROUPS):
+        for tile in tiles:
             place = PLACE[tile]
-            merged.append(
-                ((mine[place].astype(F32) + theirs[place].astype(F32)) * 0.5).astype(BF16)
+
+            @pl.when(frame < last)
+            def _():
+                pltpu.make_async_copy(mine.at[place], theirs.at[place], z_recv.at[place]).wait()
+
+            merged[tile] = (
+                (mine[place].astype(F32) + theirs[place].astype(F32)) * 0.5
+            ).astype(BF16)
+            spread = jnp.dot(
+                place_matrix, merged[tile][: 2 * CLIPS], preferred_element_type=F32
             )
-        first, tiles = unit_tiles(unit)
-        for i, block in enumerate(merged):
-            spread = jnp.dot(place_matrix, block[: 2 * CLIPS], preferred_element_type=F32)
-            outgoing[first + i] = spread.astype(BF16).reshape(RANKS, 2, LANES)
-        if tiles == 3:
-            third = jnp.concatenate([block[2 * CLIPS :] for block in merged], axis=0)
-            spread = jnp.dot(place_matrix, third, preferred_element_type=F32)
-        else:
-            spread = jnp.dot(third_matrix, merged[0][2 * CLIPS :], preferred_element_type=F32)
-            if unit == 0:
+            outgoing[PAIR_AT[tile]] = spread.astype(BF16).reshape(RANKS, 2, LANES)
+        if thirds:
+            rows = [merged[tile][2 * CLIPS :] for tile in thirds]
+            if len(rows) == 2:
+                rows = jnp.concatenate(rows, axis=0)
+                spread = jnp.dot(place_matrix, rows, preferred_element_type=F32)
+            else:
+                spread = jnp.dot(third_matrix, rows[0], preferred_element_type=F32)
                 spread = spread + count_column
-        outgoing[first + tiles - 1] = spread.astype(BF16).reshape(RANKS, 2, LANES)
-        own_copy(unit).start()
+            outgoing[first + depth - 1] = spread.astype(BF16).reshape(RANKS, 2, LANES)
+        own_copy(i).start()
 
         def send(peer):
-            at = pl.ds(first, tiles)
+            at = pl.ds(first, depth)
             pltpu.make_async_remote_copy(
-                outgoing.at[at, peer], arrived.at[at, me], x_send.at[unit], x_recv.at[unit],
+                outgoing.at[at, peer], arrived.at[at, me], x_send.at[i], x_recv.at[i],
                 device_id={"grp": peer}, device_id_type=MESH,
             ).start()
 
         for_peers(me, send, True)
 
-    def arrival(unit, sem):
-        at = pl.ds(*unit_tiles(unit))
+    def arrival(i, sem):
+        at = pl.ds(*GROUPS[i][2:])
         everyone = pl.ds(0, RANKS - 1)
         return pltpu.make_async_copy(
-            outgoing.at[at, everyone], arrived.at[at, everyone], sem.at[unit]
+            outgoing.at[at, everyone], arrived.at[at, everyone], sem.at[i]
         )
 
-    for unit in range(len(UNITS)):
-        own_copy(unit).wait()
-        arrival(unit, x_recv).wait()
-        first, tiles = unit_tiles(unit)
-        block = [arrived[first + i].reshape(2 * RANKS, LANES) for i in range(tiles)]
-        if unit == 0:
+    def slot_tile(i):
+        return arrived[i].reshape(2 * RANKS, LANES)
+
+    for i, (tiles, thirds, first, depth) in enumerate(GROUPS):
+        own_copy(i).wait()
+        arrival(i, x_recv).wait()
+        if i == 0:
             across = iota((2 * RANKS, 2 * RANKS), 1) // 2
             down = iota((2 * RANKS, 2 * RANKS), 0) // 2
             marked = iota((2 * RANKS, 2 * RANKS), 0) % 2 == 1
@@ -254,7 +262,7 @@
             same = jnp.where(marked & (down == across), 1.0, 0.0)
             table = jnp.concatenate([earlier, same], axis=1).astype(BF16)
             found = lax.dot_general(
-                block[1], table, (((0,), (0,)), ((), ())), preferred_element_type=F32
+                slot_tile(1), table, (((0,), (0,)), ((), ())), preferred_element_type=F32
             )
             opening = found[:1, : 2 * RANKS].astype(jnp.int32)
             count = found[:1, 2 * RANKS :].astype(jnp.int32)
@@ -271,15 +279,17 @@
                 jnp.concatenate([pair, third_even], axis=1).astype(BF16),
                 jnp.concatenate([pair, third_odd], axis=1).astype(BF16),
             )
-        for i, tile in enumerate(UNITS[unit]):
-            both = jnp.concatenate([block[i], block[tiles - 1]], axis=0)
-            packed = jnp.dot(pack[i], both, preferred_element_type=F32).astype(BF16)
+        if thirds:
+            shared = slot_tile(first + depth - 1)
+        for side, tile in enumerate(thirds):
+            both = jnp.concatenate([slot_tile(PAIR_AT[tile]), shared], axis=0)
+            packed = jnp.dot(pack[side], both, preferred_element_type=F32).astype(BF16)
             if tile < LEADING:
                 leading[:, tile * LANES : (tile + 1) * LANES] = packed
             else:
                 at = (tile - LEADING) * LANES
                 packed_ref[:, at : at + LANES] = packed
-        if unit == 3:
+        if i == 3:
             fetches[-1].wait()
             step = 512
             for column in range(0, OUT_WIDTH, step):
@@ -288,13 +298,13 @@
                     leading[...], weight_ref[pl.ds(0, LEAD), at], preferred_element_type=F32
                 )
 
-    for unit in range(len(UNITS)):
-        arrival(unit, x_send).wait()
+    for i in range(len(GROUPS)):
+        arrival(i, x_send).wait()
 
     @pl.when(frame > 0)
     def _():
-        for unit in range(len(UNITS)):
-            shift_copy(unit).wait_send()
+        for place in range(TILES):
+            pltpu.make_async_copy(mine.at[place], theirs.at[place], z_send.at[place]).wait()
 
 
 def project(packed_ref, live_ref, total_ref, weight_ref, bias_ref, result_ref, staged, sems):
@@ -320,7 +330,7 @@
 def shards(patch_feats, windows, counts, owners, norm_gain, norm_bias, proj_weight, proj_bias):
     vmem = pl.BlockSpec(memory_space=pltpu.VMEM)
     hbm = pl.BlockSpec(memory_space=pltpu.HBM)
-    units = len(UNITS)
+    groups = len(GROUPS)
     inputs = [
         pltpu.with_memory_space_constraint(array, pltpu.HBM)
         for array in (
@@ -348,7 +358,7 @@
             pltpu.VMEM((SLOT_TILES, RANKS, 2, LANES), BF16),
             pltpu.VMEM((ROWS, LEAD), BF16),
             pltpu.SemaphoreType.DMA((len(inputs),)),
-        ] + [pltpu.SemaphoreType.DMA((units,))] * 5,
+        ] + [pltpu.SemaphoreType.DMA((TILES,))] * 2 + [pltpu.SemaphoreType.DMA((groups,))] * 3,
         compiler_params=pltpu.CompilerParams(
             collective_id=0, has_side_effects=True, vmem_limit_bytes=24 << 20
         ),

time: 34.1 us -> 33.4 us (0.979)
  Pallas kernels: 33.9 us -> 33.2 us
    pallas_call x1, Pallas kernels: 32.5 us -> 31.8 us  [shards(): pl.pallas_call(exchange, name='exchange', out_shape=(jax.ShapeDtypeStruct...]
where the time goes in v3:
time: 33.4 us; the launch traced here: 33.2 us
  Pallas kernels  33.2 us (99%)
    pallas_call x1, Pallas kernels, shards(): pl.pallas_call(exchange, name='exchange', out_shape=(jax.ShapeDtypeStruct...  31.8 us
    pallas_call x1, Pallas kernels, shards(): pl.pallas_call(project, name='project', out_shape=jax.ShapeDtypeStruct((R...  1.44 us

profile of v3, /device:TPU:193, one launch (start us, length us, event | category | flops | bytes accessed | tf_op | source)
XLA Modules:
  0.0 33.2 jit_solution(1256644162436852739)
XLA Ops:
  0.0 0.0 copy-start
  0.0 31.8 %exchange.1 = (bf16[192,256]{1,0:T(8,128)(2,1)S(1)}, f32[192,128]{1,0:T(8,128)S(1)}, f32[192,4096]{1,0:T(8,128)S(1)}, bf16[1152,4096]{1,0:T(8,128)(2,1)S(1)}) custom-call(bf16[512,1152]{1,0:T(8,128)(2,1)} %bitcast.9, s32[3,4,64]{2,1,0:T(4,128)} %bitcast.12, s32[1,64]{1,0:T(1,128)} %counts_hbm.1, s32[1,64]{1,0:T(1,128)} %owners_hbm.1, f32[9,128]{1,0:T(8,128)} %bitcast.10, ...), custom_call_target="tpu_custom_call" | custom-call | flops 60000002048 | bytes 4000000 | tf_op jit(solution)/shard_map/exchange/pallas_call | solution.py:342
  31.8 0.0 copy-done
  31.8 1.4 %project.1 = bf16[192,4096]{1,0:T(8,128)(2,1)} custom-call(bf16[192,256]{1,0:T(8,128)(2,1)S(1)} %get-tuple-element.9.packed_ref, f32[192,128]{1,0:T(8,128)S(1)} %get-tuple-element.10.live_ref, f32[192,4096]{1,0:T(8,128)S(1)} %get-tuple-element.11.total_ref, bf16[1152,4096]{1,0:T(8,128)(2,1)S(1)} %get-tuple-element.12.weight_ref, f32[1,4096]{1,0:T(1,128)S(1)} %bitcast.8), custom_call_target="tpu_custom_call" | custom-call | flops 1811939328 | bytes 12000000 | tf_op jit(solution)/shard_map/project/pallas_call | solution.py:370
Async XLA Ops:
  0.0 31.8 %copy-start = (f32[4096]{0:T(1024)S(1)}, f32[4096]{0:T(1024)}, u32[]{:S(2)}) copy-start(f32[4096]{0:T(1024)} %param.15) | copy-start | bytes 49156

commit v4 on v3

--- a/solution.py
+++ b/solution.py
@@ -18,8 +18,8 @@
 ROWS = CLIPS * TOKENS
 TILES = WIDTH // LANES
 GROUPS = (
-    ((6,), (6,), 0, 2),
-    ((0, 3), (0, 3), 2, 3),
+    ((6,), (), 0, 1),
+    ((0, 3), (6, 0, 3), 1, 4),
     ((1, 4), (1, 4), 5, 3),
     ((2, 5), (2, 5), 8, 3),
     ((7,), (), 11, 1),
@@ -27,6 +27,7 @@
 )
 PLACE = {tile: i for i, tile in enumerate(t for group in GROUPS for t in group[0])}
 PAIR_AT = {tile: g[2] + i for g in GROUPS for i, tile in enumerate(g[0])}
+THIRD_AT = {6: 3, 0: 4, 3: 4, 1: 7, 4: 7, 2: 10, 5: 10, 7: 13, 8: 13}
 SLOT_TILES = 14
 PIECE = 32
 LEADING = 7
@@ -37,7 +38,7 @@
     return lax.broadcasted_iota(jnp.int32, shape, dim)
 
 
-def for_peers(me, act, loop):
+def for_peers(me, act):
     x, y, core = me // 16, (me // 2) % 8, me % 2
     near = [
         ((x + dx) % 4) * 16 + (core + dcore) % 2 for dx in (2, 1, 3, 0) for dcore in (0, 1)
@@ -50,11 +51,7 @@
             act(base + at)
         return carry
 
-    if loop:
-        lax.fori_loop(0, 7, row, 0)
-    else:
-        for i in range(7):
-            row(i, 0)
+    lax.fori_loop(0, 7, row, 0)
     for i in (0, 1, 2, 3, 4, 5, 7):
         act(near[i] + 2 * y)
 
@@ -64,7 +61,7 @@
     packed_ref, live_ref, total_ref, weight_ref,
     feats, win_ref, counts_ref, owners_ref, gain_ref, bias_ref,
     stats, mine, theirs, outgoing, arrived, leading,
-    fetch_sem, z_send, z_recv, x_send, x_recv, own_sem,
+    fetch_sem, z_send, z_recv, x_send, x_recv, own_sem, column_sem, row_sem,
 ):
     me = lax.axis_index("grp")
     frame = lax.axis_index("enc")
@@ -85,10 +82,18 @@
     before = jnp.maximum(frame - 1, 0)
     after = jnp.minimum(frame + 1, last)
 
-    def greet(peer):
-        pl.semaphore_signal(barrier, inc=1, device_id={"grp": peer}, device_id_type=MESH)
-
-    for_peers(me, greet, False)
+    x, y, core = me // 16, (me // 2) % 8, me % 2
+    column_peers = [16 * x + 2 * ((y + dy) % 8) + core for dy in (2, 6, 1, 7)]
+    row_peers = [
+        16 * ((x + dx) % 4) + 2 * y + (core + dcore) % 2
+        for dx, dcore in ((2, 1), (2, 0), (1, 1), (3, 1), (1, 0), (3, 0), (0, 1))
+    ]
+
+    def tell(sem, peers):
+        for peer in peers:
+            pl.semaphore_signal(sem, inc=1, device_id={"grp": peer}, device_id_type=MESH)
+
+    tell(barrier, column_peers + row_peers)
 
     @pl.when(frame > 0)
     def _():
@@ -113,7 +118,7 @@
         stats[1, at, :] = jnp.broadcast_to(lax.rsqrt(var + 1e-6), (group, LANES))
         return carry
 
-    lax.fori_loop(0, CLIPS * PATCHES // group, statistics, 0)
+    lax.fori_loop(0, CLIPS * PATCHES // group, statistics, 0, unroll=2)
     diagonal = iota((LANES, LANES), 0) == iota((LANES, LANES), 1)
 
     def as_row(which, start):
@@ -184,52 +189,75 @@
     count_column = jnp.sum(odd_rows * count_row, axis=1, keepdims=True)
 
     neighbours = jnp.minimum(frame, 1) + jnp.minimum(last - frame, 1)
-    pl.semaphore_wait(barrier, RANKS - 1 + neighbours)
+    pl.semaphore_wait(barrier, len(column_peers) + len(row_peers) + neighbours)
+    tell(column_sem, column_peers)
 
     pieces = ROWS // PIECE
+    parts = [(0, 2 * CLIPS, 0), (0, CLIPS, TILES)] + [(p, ROWS, p) for p in range(1, TILES)]
+
+    def shift(place, piece, sem):
+        at = pl.ds(pl.multiple_of(piece * PIECE, PIECE), PIECE)
+        pltpu.make_async_remote_copy(
+            mine.at[place, at], theirs.at[place, at], z_send.at[sem], z_recv.at[sem],
+            device_id={"enc": before}, device_id_type=MESH,
+        ).start()
 
     @pl.when(frame > 0)
     def _():
-        def shift(i, carry):
-            place = i // pieces
-            at = pl.ds(pl.multiple_of((i % pieces) * PIECE, PIECE), PIECE)
-            pltpu.make_async_remote_copy(
-                mine.at[place, at], theirs.at[place, at], z_send.at[place], z_recv.at[place],
-                device_id={"enc": before}, device_id_type=MESH,
-            ).start()
+        pairs_end = 2 * CLIPS // PIECE
+        for piece in range(pieces):
+            shift(0, piece, 0 if piece < pairs_end else TILES)
+
+        def rest(i, carry):
+            shift(i // pieces, i % pieces, i // pieces)
             return carry
 
-        lax.fori_loop(0, TILES * pieces, shift, 0)
+        lax.fori_loop(pieces, TILES * pieces, rest, 0)
+
+    pl.semaphore_wait(column_sem, len(column_peers))
+    tell(row_sem, row_peers)
+    pl.semaphore_wait(row_sem, len(row_peers))
+
+    def shift_wait(part, sems):
+        place, rows, sem = parts[part]
+        at = pl.ds(0, rows)
+        pltpu.make_async_copy(mine.at[place, at], theirs.at[place, at], sems.at[sem]).wait()
+
+    def shifted(part):
+        @pl.when(frame < last)
+        def _():
+            shift_wait(part, z_recv)
+
+    def merge(place, at):
+        return ((mine[place, at, :].astype(F32) + theirs[place, at, :].astype(F32)) * 0.5).astype(
+            BF16
+        )
+
+    def lay_out(matrix, rows):
+        return jnp.dot(matrix, rows, preferred_element_type=F32)
+
+    def put(at, spread):
+        outgoing[at] = spread.astype(BF16).reshape(RANKS, 2, LANES)
 
     def own_copy(i):
         at = pl.ds(*GROUPS[i][2:])
         return pltpu.make_async_copy(outgoing.at[at, me], arrived.at[at, me], own_sem.at[i])
 
-    merged = {}
+    thirds_of = {}
+    first_two, third_rows = pl.ds(0, 2 * CLIPS), pl.ds(2 * CLIPS, CLIPS)
     for i, (tiles, thirds, first, depth) in enumerate(GROUPS):
         for tile in tiles:
             place = PLACE[tile]
-
-            @pl.when(frame < last)
-            def _():
-                pltpu.make_async_copy(mine.at[place], theirs.at[place], z_recv.at[place]).wait()
-
-            merged[tile] = (
-                (mine[place].astype(F32) + theirs[place].astype(F32)) * 0.5
-            ).astype(BF16)
-            spread = jnp.dot(
-                place_matrix, merged[tile][: 2 * CLIPS], preferred_element_type=F32
-            )
-            outgoing[PAIR_AT[tile]] = spread.astype(BF16).reshape(RANKS, 2, LANES)
+            shifted(place + 1 if place else 0)
+            put(PAIR_AT[tile], lay_out(place_matrix, merge(place, first_two)))
+            if place:
+                thirds_of[tile] = merge(place, third_rows)
+        if i == 1:
+            shifted(1)
+            put(THIRD_AT[6], lay_out(third_matrix, merge(0, third_rows)) + count_column)
         if thirds:
-            rows = [merged[tile][2 * CLIPS :] for tile in thirds]
-            if len(rows) == 2:
-                rows = jnp.concatenate(rows, axis=0)
-                spread = jnp.dot(place_matrix, rows, preferred_element_type=F32)
-            else:
-                spread = jnp.dot(third_matrix, rows[0], preferred_element_type=F32)
-                spread = spread + count_column
-            outgoing[first + depth - 1] = spread.astype(BF16).reshape(RANKS, 2, LANES)
+            rows = jnp.concatenate([thirds_of[tile] for tile in thirds[-2:]], axis=0)
+            put(THIRD_AT[thirds[-1]], lay_out(place_matrix, rows))
         own_copy(i).start()
 
         def send(peer):
@@ -239,7 +267,7 @@
                 device_id={"grp": peer}, device_id_type=MESH,
             ).start()
 
-        for_peers(me, send, True)
+        for_peers(me, send)
 
     def arrival(i, sem):
         at = pl.ds(*GROUPS[i][2:])
@@ -254,7 +282,7 @@
     for i, (tiles, thirds, first, depth) in enumerate(GROUPS):
         own_copy(i).wait()
         arrival(i, x_recv).wait()
-        if i == 0:
+        if i == 1:
             across = iota((2 * RANKS, 2 * RANKS), 1) // 2
             down = iota((2 * RANKS, 2 * RANKS), 0) // 2
             marked = iota((2 * RANKS, 2 * RANKS), 0) % 2 == 1
@@ -262,7 +290,7 @@
             same = jnp.where(marked & (down == across), 1.0, 0.0)
             table = jnp.concatenate([earlier, same], axis=1).astype(BF16)
             found = lax.dot_general(
-                slot_tile(1), table, (((0,), (0,)), ((), ())), preferred_element_type=F32
+                slot_tile(THIRD_AT[6]), table, (((0,), (0,)), ((), ())), preferred_element_type=F32
             )
             opening = found[:1, : 2 * RANKS].astype(jnp.int32)
             count = found[:1, 2 * RANKS :].astype(jnp.int32)
@@ -279,10 +307,11 @@
                 jnp.concatenate([pair, third_even], axis=1).astype(BF16),
                 jnp.concatenate([pair, third_odd], axis=1).astype(BF16),
             )
-        if thirds:
-            shared = slot_tile(first + depth - 1)
-        for side, tile in enumerate(thirds):
-            both = jnp.concatenate([slot_tile(PAIR_AT[tile]), shared], axis=0)
+        for tile in thirds:
+            side = tile in (3, 4, 5, 8)
+            both = jnp.concatenate(
+                [slot_tile(PAIR_AT[tile]), slot_tile(THIRD_AT[tile])], axis=0
+            )
             packed = jnp.dot(pack[side], both, preferred_element_type=F32).astype(BF16)
             if tile < LEADING:
                 leading[:, tile * LANES : (tile + 1) * LANES] = packed
@@ -303,8 +332,8 @@
 
     @pl.when(frame > 0)
     def _():
-        for place in range(TILES):
-            pltpu.make_async_copy(mine.at[place], theirs.at[place], z_send.at[place]).wait()
+        for part in range(len(parts)):
+            shift_wait(part, z_send)
 
 
 def project(packed_ref, live_ref, total_ref, weight_ref, bias_ref, result_ref, staged, sems):
@@ -358,7 +387,9 @@
             pltpu.VMEM((SLOT_TILES, RANKS, 2, LANES), BF16),
             pltpu.VMEM((ROWS, LEAD), BF16),
             pltpu.SemaphoreType.DMA((len(inputs),)),
-        ] + [pltpu.SemaphoreType.DMA((TILES,))] * 2 + [pltpu.SemaphoreType.DMA((groups,))] * 3,
+        ] + [pltpu.SemaphoreType.DMA((TILES + 1,))] * 2 + [
+            pltpu.SemaphoreType.DMA((groups,))
+        ] * 3 + [pltpu.SemaphoreType.REGULAR] * 2,
         compiler_params=pltpu.CompilerParams(
             collective_id=0, has_side_effects=True, vmem_limit_bytes=24 << 20
         ),

time: 33.4 us -> 34.7 us (1.039)
  the two profiles are of different devices: /device:TPU:193 before, /device:TPU:1 now
where the time goes in v4:
time: 34.7 us; the launch traced here: 34.5 us
  Pallas kernels  34.5 us (99%)
    pallas_call x1, Pallas kernels, shards(): pl.pallas_call(exchange, name='exchange', out_shape=(jax.ShapeDtypeStruct...  33 us
    pallas_call x1, Pallas kernels, shards(): pl.pallas_call(project, name='project', out_shape=jax.ShapeDtypeStruct((R...  1.44 us

profile of v4, /device:TPU:1, one launch (start us, length us, event | category | flops | bytes accessed | tf_op | source)
XLA Modules:
  0.0 34.5 jit_solution(9763217557753911928)
XLA Ops:
  0.0 0.0 copy-start
  0.0 33.0 %exchange.1 = (bf16[192,256]{1,0:T(8,128)(2,1)S(1)}, f32[192,128]{1,0:T(8,128)S(1)}, f32[192,4096]{1,0:T(8,128)S(1)}, bf16[1152,4096]{1,0:T(8,128)(2,1)S(1)}) custom-call(bf16[512,1152]{1,0:T(8,128)(2,1)} %bitcast.9, s32[3,4,64]{2,1,0:T(4,128)} %bitcast.12, s32[1,64]{1,0:T(1,128)} %counts_hbm.1, s32[1,64]{1,0:T(1,128)} %owners_hbm.1, f32[9,128]{1,0:T(8,128)} %bitcast.10, ...), custom_call_target="tpu_custom_call" | custom-call | flops 60000002048 | bytes 4000000 | tf_op jit(solution)/shard_map/exchange/pallas_call | solution.py:371
  33.0 0.0 copy-done
  33.1 1.4 %project.1 = bf16[192,4096]{1,0:T(8,128)(2,1)} custom-call(bf16[192,256]{1,0:T(8,128)(2,1)S(1)} %get-tuple-element.9.packed_ref, f32[192,128]{1,0:T(8,128)S(1)} %get-tuple-element.10.live_ref, f32[192,4096]{1,0:T(8,128)S(1)} %get-tuple-element.11.total_ref, bf16[1152,4096]{1,0:T(8,128)(2,1)S(1)} %get-tuple-element.12.weight_ref, f32[1,4096]{1,0:T(1,128)S(1)} %bitcast.8), custom_call_target="tpu_custom_call" | custom-call | flops 1811939328 | bytes 12000000 | tf_op jit(solution)/shard_map/project/pallas_call | solution.py:401
Async XLA Ops:
  0.0 33.0 %copy-start = (f32[4096]{0:T(1024)S(1)}, f32[4096]{0:T(1024)}, u32[]{:S(2)}) copy-start(f32[4096]{0:T(1024)} %param.15) | copy-start | bytes 49156

commit v5 on v4

--- a/solution.py
+++ b/solution.py
@@ -93,7 +93,32 @@
         for peer in peers:
             pl.semaphore_signal(sem, inc=1, device_id={"grp": peer}, device_id_type=MESH)
 
-    tell(barrier, column_peers + row_peers)
+    outer = frame > 0
+    everyone = RANKS - 1
+
+    def tell_plane(sem, condition):
+        def signal(peer):
+            @pl.when(peer != 0)
+            def _():
+                tell(sem, [peer])
+
+        @pl.when(condition)
+        def _():
+            for_peers(me, signal)
+
+    @pl.when(outer)
+    def _():
+        tell(barrier, column_peers + row_peers)
+
+    @pl.when((frame == 0) & (me > 0))
+    def _():
+        tell(barrier, [0])
+
+    @pl.when((frame == 0) & (me == 0))
+    def _():
+        tell(barrier, [1])
+
+    tell_plane(barrier, (frame == 0) & (me > 0))
 
     @pl.when(frame > 0)
     def _():
@@ -189,8 +214,17 @@
     count_column = jnp.sum(odd_rows * count_row, axis=1, keepdims=True)
 
     neighbours = jnp.minimum(frame, 1) + jnp.minimum(last - frame, 1)
-    pl.semaphore_wait(barrier, len(column_peers) + len(row_peers) + neighbours)
-    tell(column_sem, column_peers)
+    late = (frame == 0) & (me > 1)
+    greetings = jnp.where(
+        outer, len(column_peers) + len(row_peers), jnp.where(late, everyone - 1, everyone)
+    )
+    pl.semaphore_wait(barrier, greetings + neighbours)
+
+    @pl.when(outer)
+    def _():
+        tell(column_sem, column_peers)
+
+    tell_plane(row_sem, (frame == 0) & (me == 1))
 
     pieces = ROWS // PIECE
     parts = [(0, 2 * CLIPS, 0), (0, CLIPS, TILES)] + [(p, ROWS, p) for p in range(1, TILES)]
@@ -214,9 +248,13 @@
 
         lax.fori_loop(pieces, TILES * pieces, rest, 0)
 
-    pl.semaphore_wait(column_sem, len(column_peers))
-    tell(row_sem, row_peers)
-    pl.semaphore_wait(row_sem, len(row_peers))
+    @pl.when(outer)
+    def _():
+        pl.semaphore_wait(column_sem, len(column_peers))
+        tell(row_sem, row_peers)
+        pl.semaphore_wait(row_sem, len(row_peers))
+
+    held = jnp.where(late, 0, -1)
 
     def shift_wait(part, sems):
         place, rows, sem = parts[part]
@@ -242,6 +280,13 @@
     def own_copy(i):
         at = pl.ds(*GROUPS[i][2:])
         return pltpu.make_async_copy(outgoing.at[at, me], arrived.at[at, me], own_sem.at[i])
+
+    def send(i, peer):
+        at = pl.ds(*GROUPS[i][2:])
+        pltpu.make_async_remote_copy(
+            outgoing.at[at, peer], arrived.at[at, me], x_send.at[i], x_recv.at[i],
+            device_id={"grp": peer}, device_id_type=MESH,
+        ).start()
 
     thirds_of = {}
     first_two, third_rows = pl.ds(0, 2 * CLIPS), pl.ds(2 * CLIPS, CLIPS)
@@ -260,21 +305,23 @@
             put(THIRD_AT[thirds[-1]], lay_out(place_matrix, rows))
         own_copy(i).start()
 
-        def send(peer):
-            at = pl.ds(first, depth)
-            pltpu.make_async_remote_copy(
-                outgoing.at[at, peer], arrived.at[at, me], x_send.at[i], x_recv.at[i],
-                device_id={"grp": peer}, device_id_type=MESH,
-            ).start()
-
-        for_peers(me, send)
+        def send_unheld(peer):
+            @pl.when(peer != held)
+            def _():
+                send(i, peer)
+
+        for_peers(me, send_unheld)
+
+    @pl.when(late)
+    def _():
+        pl.semaphore_wait(row_sem, 1)
+        for i in range(len(GROUPS)):
+            send(i, 0)
 
     def arrival(i, sem):
         at = pl.ds(*GROUPS[i][2:])
-        everyone = pl.ds(0, RANKS - 1)
-        return pltpu.make_async_copy(
-            outgoing.at[at, everyone], arrived.at[at, everyone], sem.at[i]
-        )
+        others = pl.ds(0, RANKS - 1)
+        return pltpu.make_async_copy(outgoing.at[at, others], arrived.at[at, others], sem.at[i])
 
     def slot_tile(i):
         return arrived[i].reshape(2 * RANKS, LANES)

time: 34.7 us -> 32.4 us (0.934)
  the two profiles are of different devices: /device:TPU:1 before, /device:TPU:193 now
where the time goes in v5:
time: 32.4 us; the launch traced here: 32.3 us
  Pallas kernels  32.2 us (99%)
    pallas_call x1, Pallas kernels, shards(): pl.pallas_call(exchange, name='exchange', out_shape=(jax.ShapeDtypeStruct...  30.8 us
    pallas_call x1, Pallas kernels, shards(): pl.pallas_call(project, name='project', out_shape=jax.ShapeDtypeStruct((R...  1.44 us

profile of v5, /device:TPU:193, one launch (start us, length us, event | category | flops | bytes accessed | tf_op | source)
XLA Modules:
  0.0 32.3 jit_solution(8937308464318923889)
XLA Ops:
  0.0 0.0 copy-start
  0.0 30.8 %exchange.1 = (bf16[192,256]{1,0:T(8,128)(2,1)S(1)}, f32[192,128]{1,0:T(8,128)S(1)}, f32[192,4096]{1,0:T(8,128)S(1)}, bf16[1152,4096]{1,0:T(8,128)(2,1)S(1)}) custom-call(bf16[512,1152]{1,0:T(8,128)(2,1)} %bitcast.9, s32[3,4,64]{2,1,0:T(4,128)} %bitcast.12, s32[1,64]{1,0:T(1,128)} %counts_hbm.1, s32[1,64]{1,0:T(1,128)} %owners_hbm.1, f32[9,128]{1,0:T(8,128)} %bitcast.10, ...), custom_call_target="tpu_custom_call" | custom-call | flops 60000002048 | bytes 4000000 | tf_op jit(solution)/shard_map/exchange/pallas_call | solution.py:418
  30.8 0.0 copy-done
  30.8 1.4 %project.1 = bf16[192,4096]{1,0:T(8,128)(2,1)} custom-call(bf16[192,256]{1,0:T(8,128)(2,1)S(1)} %get-tuple-element.9.packed_ref, f32[192,128]{1,0:T(8,128)S(1)} %get-tuple-element.10.live_ref, f32[192,4096]{1,0:T(8,128)S(1)} %get-tuple-element.11.total_ref, bf16[1152,4096]{1,0:T(8,128)(2,1)S(1)} %get-tuple-element.12.weight_ref, f32[1,4096]{1,0:T(1,128)S(1)} %bitcast.8), custom_call_target="tpu_custom_call" | custom-call | flops 1811939328 | bytes 12000000 | tf_op jit(solution)/shard_map/project/pallas_call | solution.py:448
Async XLA Ops:
  0.0 30.8 %copy-start = (f32[4096]{0:T(1024)S(1)}, f32[4096]{0:T(1024)}, u32[]{:S(2)}) copy-start(f32[4096]{0:T(1024)} %param.15) | copy-start | bytes 49156

commit v6 on v5

--- a/solution.py
+++ b/solution.py
@@ -18,8 +18,8 @@
 ROWS = CLIPS * TOKENS
 TILES = WIDTH // LANES
 GROUPS = (
-    ((6,), (), 0, 1),
-    ((0, 3), (6, 0, 3), 1, 4),
+    ((6,), (6,), 0, 2),
+    ((0, 3), (0, 3), 2, 3),
     ((1, 4), (1, 4), 5, 3),
     ((2, 5), (2, 5), 8, 3),
     ((7,), (), 11, 1),
@@ -27,7 +27,7 @@
 )
 PLACE = {tile: i for i, tile in enumerate(t for group in GROUPS for t in group[0])}
 PAIR_AT = {tile: g[2] + i for g in GROUPS for i, tile in enumerate(g[0])}
-THIRD_AT = {6: 3, 0: 4, 3: 4, 1: 7, 4: 7, 2: 10, 5: 10, 7: 13, 8: 13}
+THIRD_AT = {6: 1, 0: 4, 3: 4, 1: 7, 4: 7, 2: 10, 5: 10, 7: 13, 8: 13}
 SLOT_TILES = 14
 PIECE = 32
 LEADING = 7
@@ -66,8 +66,9 @@
     me = lax.axis_index("grp")
     frame = lax.axis_index("enc")
     last = lax.axis_size("enc") - 1
+    quarter = pl.ds(0, CLIPS * PATCHES // 4)
     pairs = (
-        (feats_hbm, feats), (win_hbm, win_ref), (counts_hbm, counts_ref),
+        (feats_hbm.at[quarter], feats.at[quarter]), (win_hbm, win_ref), (counts_hbm, counts_ref),
         (owners_hbm, owners_ref), (gain_hbm, gain_ref), (bias_hbm, bias_ref),
         (weight_hbm, weight_ref),
     )
@@ -75,6 +76,14 @@
         pltpu.make_async_copy(source, target, fetch_sem.at[i])
         for i, (source, target) in enumerate(pairs)
     ]
+    for i in range(1, 4):
+        quarter = pl.ds(i * CLIPS * PATCHES // 4, CLIPS * PATCHES // 4)
+        fetches.insert(
+            i,
+            pltpu.make_async_copy(
+                feats_hbm.at[quarter], feats.at[quarter], fetch_sem.at[len(pairs) + i - 1]
+            ),
+        )
     for fetch in fetches[:-1]:
         fetch.start()
 
@@ -128,9 +137,6 @@
     def _():
         pl.semaphore_signal(barrier, inc=1, device_id={"enc": after}, device_id_type=MESH)
 
-    for fetch in fetches[:-1]:
-        fetch.wait()
-    fetches[-1].start()
     group = 32
 
     def statistics(i, carry):
@@ -143,7 +149,13 @@
         stats[1, at, :] = jnp.broadcast_to(lax.rsqrt(var + 1e-6), (group, LANES))
         return carry
 
-    lax.fori_loop(0, CLIPS * PATCHES // group, statistics, 0, unroll=2)
+    steps = CLIPS * PATCHES // group // 4
+    for i in range(4):
+        fetches[i].wait()
+        lax.fori_loop(i * steps, (i + 1) * steps, statistics, 0, unroll=2)
+    fetches[-1].start()
+    for fetch in fetches[4:-1]:
+        fetch.wait()
     diagonal = iota((LANES, LANES), 0) == iota((LANES, LANES), 1)
 
     def as_row(which, start):
@@ -227,44 +239,34 @@
     tell_plane(row_sem, (frame == 0) & (me == 1))
 
     pieces = ROWS // PIECE
-    parts = [(0, 2 * CLIPS, 0), (0, CLIPS, TILES)] + [(p, ROWS, p) for p in range(1, TILES)]
-
-    def shift(place, piece, sem):
-        at = pl.ds(pl.multiple_of(piece * PIECE, PIECE), PIECE)
-        pltpu.make_async_remote_copy(
-            mine.at[place, at], theirs.at[place, at], z_send.at[sem], z_recv.at[sem],
-            device_id={"enc": before}, device_id_type=MESH,
-        ).start()
 
     @pl.when(frame > 0)
     def _():
-        pairs_end = 2 * CLIPS // PIECE
-        for piece in range(pieces):
-            shift(0, piece, 0 if piece < pairs_end else TILES)
-
-        def rest(i, carry):
-            shift(i // pieces, i % pieces, i // pieces)
+        def shift(i, carry):
+            place = i // pieces
+            at = pl.ds(pl.multiple_of((i % pieces) * PIECE, PIECE), PIECE)
+            pltpu.make_async_remote_copy(
+                mine.at[place, at], theirs.at[place, at], z_send.at[place], z_recv.at[place],
+                device_id={"enc": before}, device_id_type=MESH,
+            ).start()
             return carry
 
-        lax.fori_loop(pieces, TILES * pieces, rest, 0)
+        lax.fori_loop(0, TILES * pieces, shift, 0)
 
     @pl.when(outer)
     def _():
         pl.semaphore_wait(column_sem, len(column_peers))
         tell(row_sem, row_peers)
-        pl.semaphore_wait(row_sem, len(row_peers))
 
     held = jnp.where(late, 0, -1)
 
-    def shift_wait(part, sems):
-        place, rows, sem = parts[part]
-        at = pl.ds(0, rows)
-        pltpu.make_async_copy(mine.at[place, at], theirs.at[place, at], sems.at[sem]).wait()
-
-    def shifted(part):
+    def shift_wait(place, sems):
+        pltpu.make_async_copy(mine.at[place], theirs.at[place], sems.at[place]).wait()
+
+    def shifted(place):
         @pl.when(frame < last)
         def _():
-            shift_wait(part, z_recv)
+            shift_wait(place, z_recv)
 
     def merge(place, at):
         return ((mine[place, at, :].astype(F32) + theirs[place, at, :].astype(F32)) * 0.5).astype(
@@ -293,17 +295,19 @@
     for i, (tiles, thirds, first, depth) in enumerate(GROUPS):
         for tile in tiles:
             place = PLACE[tile]
-            shifted(place + 1 if place else 0)
+            shifted(place)
             put(PAIR_AT[tile], lay_out(place_matrix, merge(place, first_two)))
-            if place:
-                thirds_of[tile] = merge(place, third_rows)
-        if i == 1:
-            shifted(1)
-            put(THIRD_AT[6], lay_out(third_matrix, merge(0, third_rows)) + count_column)
-        if thirds:
-            rows = jnp.concatenate([thirds_of[tile] for tile in thirds[-2:]], axis=0)
+            thirds_of[tile] = merge(place, third_rows)
+        if i == 0:
+            put(THIRD_AT[6], lay_out(third_matrix, thirds_of[6]) + count_column)
+        elif thirds:
+            rows = jnp.concatenate([thirds_of[tile] for tile in thirds], axis=0)
             put(THIRD_AT[thirds[-1]], lay_out(place_matrix, rows))
         own_copy(i).start()
+        if i == 0:
+            @pl.when(outer)
+            def _():
+                pl.semaphore_wait(row_sem, len(row_peers))
 
         def send_unheld(peer):
             @pl.when(peer != held)
@@ -329,7 +333,7 @@
     for i, (tiles, thirds, first, depth) in enumerate(GROUPS):
         own_copy(i).wait()
         arrival(i, x_recv).wait()
-        if i == 1:
+        if i == 0:
             across = iota((2 * RANKS, 2 * RANKS), 1) // 2
             down = iota((2 * RANKS, 2 * RANKS), 0) // 2
             marked = iota((2 * RANKS, 2 * RANKS), 0) % 2 == 1
@@ -379,8 +383,8 @@
 
     @pl.when(frame > 0)
     def _():
-        for part in range(len(parts)):
-            shift_wait(part, z_send)
+        for place in range(TILES):
+            shift_wait(place, z_send)
 
 
 def project(packed_ref, live_ref, total_ref, weight_ref, bias_ref, result_ref, staged, sems):
@@ -433,8 +437,8 @@
             pltpu.VMEM((SLOT_TILES, RANKS, 2, LANES), BF16),
             pltpu.VMEM((SLOT_TILES, RANKS, 2, LANES), BF16),
             pltpu.VMEM((ROWS, LEAD), BF16),
-            pltpu.SemaphoreType.DMA((len(inputs),)),
-        ] + [pltpu.SemaphoreType.DMA((TILES + 1,))] * 2 + [
+            pltpu.SemaphoreType.DMA((len(inputs) + 3,)),
+        ] + [pltpu.SemaphoreType.DMA((TILES,))] * 2 + [
             pltpu.SemaphoreType.DMA((groups,))
         ] * 3 + [pltpu.SemaphoreType.REGULAR] * 2,
         compiler_params=pltpu.CompilerParams(

time: 32.4 us -> 31.8 us (0.981)
  Pallas kernels: 32.2 us -> 31.6 us
    pallas_call x1, Pallas kernels: 30.8 us -> 30.2 us  [shards(): pl.pallas_call(exchange, name='exchange', out_shape=(jax.ShapeDtypeStruct...]
where the time goes in v6:
time: 31.8 us; the launch traced here: 31.6 us
  Pallas kernels  31.6 us (99%)
    pallas_call x1, Pallas kernels, shards(): pl.pallas_call(exchange, name='exchange', out_shape=(jax.ShapeDtypeStruct...  30.2 us
    pallas_call x1, Pallas kernels, shards(): pl.pallas_call(project, name='project', out_shape=jax.ShapeDtypeStruct((R...  1.44 us

profile of v6, /device:TPU:193, one launch (start us, length us, event | category | flops | bytes accessed | tf_op | source)
XLA Modules:
  0.0 31.6 jit_solution(14025864771177708840)
XLA Ops:
  0.0 0.0 copy-start
  0.0 30.2 %exchange.1 = (bf16[192,256]{1,0:T(8,128)(2,1)S(1)}, f32[192,128]{1,0:T(8,128)S(1)}, f32[192,4096]{1,0:T(8,128)S(1)}, bf16[1152,4096]{1,0:T(8,128)(2,1)S(1)}) custom-call(bf16[512,1152]{1,0:T(8,128)(2,1)} %bitcast.9, s32[3,4,64]{2,1,0:T(4,128)} %bitcast.12, s32[1,64]{1,0:T(1,128)} %counts_hbm.1, s32[1,64]{1,0:T(1,128)} %owners_hbm.1, f32[9,128]{1,0:T(8,128)} %bitcast.10, ...), custom_call_target="tpu_custom_call" | custom-call | flops 60000002048 | bytes 4000000 | tf_op jit(solution)/shard_map/exchange/pallas_call | solution.py:422
  30.2 0.0 copy-done
  30.2 1.4 %project.1 = bf16[192,4096]{1,0:T(8,128)(2,1)} custom-call(bf16[192,256]{1,0:T(8,128)(2,1)S(1)} %get-tuple-element.9.packed_ref, f32[192,128]{1,0:T(8,128)S(1)} %get-tuple-element.10.live_ref, f32[192,4096]{1,0:T(8,128)S(1)} %get-tuple-element.11.total_ref, bf16[1152,4096]{1,0:T(8,128)(2,1)S(1)} %get-tuple-element.12.weight_ref, f32[1,4096]{1,0:T(1,128)S(1)} %bitcast.8), custom_call_target="tpu_custom_call" | custom-call | flops 1811939328 | bytes 12000000 | tf_op jit(solution)/shard_map/project/pallas_call | solution.py:452
Async XLA Ops:
  0.0 30.2 %copy-start = (f32[4096]{0:T(1024)S(1)}, f32[4096]{0:T(1024)}, u32[]{:S(2)}) copy-start(f32[4096]{0:T(1024)} %param.15) | copy-start | bytes 49156
